TPU v7x, 128 devices: a whole 4x4x4 slice. The times are simulated.
128 devices in a mesh: seq: 64 (over x, z, y), head: 2 (over core).
Axes of the slice: x: 4, y: 4, z: 4, core: 2. Of those that a mesh axis runs over, the one named last changes fastest.
Arguments:
- queries: bfloat16 [16384, 4096], P('seq', 'head'), may hold values from -210 to 210
- keys: bfloat16 [16384, 1024], P('seq', 'head'), may hold values from -7 to 7
- values: bfloat16 [16384, 1024], P('seq', 'head'), may hold values from -6 to 6
- vertical: int32 [8, 64], P('head'), may hold values from 0 to 255, as said below
- slash: int32 [8, 2], P('head'), may hold values from 1 to 4, as said below
- out_weight: bfloat16 [4096, 4096], P('head'), may hold values from -1 to 1
Outputs:
- mixed: bfloat16 [16384, 4096], P(('seq', 'head'))
Inputs may be any that keep to these rules, and one draw needn't show every extreme that they name: `vertical`: for each key-value head, 64 different key blocks in increasing order; block b lies in slab b // 4; no slab holds more than 2 of one head's blocks, and for every head some slab holds exactly 2. `slash`: for each key-value head, 2 different offsets in increasing order; some head has the offset 256 // 64.
All inputs are finite; a program needn't handle non-finite values.
Results may differ from a plain program's by a relative error of at most 0.01.
Values may be sent and summed in bfloat16 or wider, within the bound.
A program may use at most 128 MiB of HBM per device.

v0:
```python
import functools
import math

import jax
import jax.numpy as jnp
from jax import lax
from jax.experimental import pallas as pl
from jax.experimental.pallas import tpu as pltpu
from jax.sharding import PartitionSpec as P

HEAD_DIM = 128
BLK = 64
CAP = 2
NEGATIVE = -1e30
MESH = pl.DeviceIdType.MESH
SCALE = HEAD_DIM ** (-0.5) * math.log2(math.e)


def kernel(
    n, inner, cut, kv, per_group, tile,
    q_ref, k_ref, v_ref, vert_ref, slash_ref, w_hbm, out_ref,
    pack_ref, bias_ref, slots, prev, w_ref, acc, top, total, attn, res, give, take,
    w_sem, prev_send, prev_recv, slot_recv, k_up, k_in, v_in, v_up, x_send, x_recv,
):
    rows = q_ref.shape[0]
    outer = n // inner
    me = lax.axis_index("seq")
    core = lax.axis_index("head")
    o, c = me // inner, me % inner
    other = 1 - core
    slab_blocks = rows // BLK
    half = rows // 2
    slot_keys = CAP * BLK

    barrier = pltpu.get_barrier_semaphore()

    def greet(seq, head):
        pl.semaphore_signal(barrier, inc=1, device_id=(seq, head), device_id_type=MESH)

    greet(me, other)
    for d in range(1, inner):
        greet(o * inner + (c + d) % inner, core)
    if outer > 1:
        greet((me + inner) % n, core)
        greet((me + n - inner) % n, core)

    @pl.when(me + 1 < n)
    def _():
        greet(me + 1, core)

    @pl.when(me > 0)
    def _():
        greet(me - 1, core)

    first_block = me * slab_blocks
    none = n * slab_blocks
    chosen_count = vert_ref.shape[1]
    for h in range(kv):
        low, high = jnp.int32(none), jnp.int32(-1)
        for i in range(chosen_count):
            block = vert_ref[h, i] - first_block
            inside = (block >= 0) & (block < slab_blocks)
            low = jnp.where(inside, jnp.minimum(low, block), low)
            high = jnp.where(inside, jnp.maximum(high, block), high)
        columns = slice(h * HEAD_DIM, (h + 1) * HEAD_DIM)
        for part, source in enumerate((k_ref, v_ref)):
            for slot, pick in enumerate((low, high)):
                got = source[:BLK, columns]
                for i in range(1, slab_blocks):
                    got = jnp.where(pick == i, source[i * BLK:(i + 1) * BLK, columns], got)
                at = part * slot_keys + slot * BLK
                pack_ref[at:at + BLK, columns] = got

    weight_copy = pltpu.make_async_copy(w_hbm, w_ref, w_sem)
    weight_copy.start()
    pl.semaphore_wait(
        barrier,
        1 + (inner - 1) + (2 if outer > 1 else 0) + jnp.where(me > 0, 1, 0) + jnp.where(me + 1 < n, 1, 0),
    )

    def remote(src, dst, send_sem, recv_sem, seq):
        return pltpu.make_async_remote_copy(
            src_ref=src, dst_ref=dst, send_sem=send_sem, recv_sem=recv_sem,
            device_id=(seq, core), device_id_type=MESH,
        )

    parts = (pl.ds(0, cut), pl.ds(cut, 2 * slot_keys - cut))
    above = (me + inner) % n

    def relay(slab, part, send_sem, seq, own=False):
        there = slots.at[slab, parts[part]]
        return remote(pack_ref.at[parts[part]] if own else there, there, send_sem,
                      slot_recv.at[slab, part], seq)

    def arrived(slab, part):
        relay(slab, part, k_up.at[0], above).wait_recv()

    def own_plane(act):
        for d in range(1, inner):
            peer = (c + d) % inner

            @pl.when((o < outer - 1) | (peer > c))
            def _(d=d, peer=peer):
                act(relay(me, 1, v_in.at[d], o * inner + peer, own=True))

        @pl.when(o < outer - 1)
        def _():
            act(relay(me, 0, k_up.at[0], above, own=True))

        for d in range(1, inner):
            peer = (c + d) % inner

            @pl.when(peer > c)
            def _(d=d, peer=peer):
                act(relay(me, 0, k_in.at[0, d], o * inner + peer, own=True))

        @pl.when(o < outer - 1)
        def _():
            act(relay(me, 1, v_up.at[0, 0], above, own=True))

        @pl.when(me + 1 < n)
        def _():
            for i, own in enumerate((k_ref, v_ref)):
                act(remote(own, prev.at[i], prev_send.at[i], prev_recv.at[i], me + 1))

    def spread_plane(d, start):
        act = (lambda copy: copy.start()) if start else (lambda copy: copy.wait_send())
        source = me - d * inner
        if start:
            arrived(source, 0)

        @pl.when(o < outer - 1)
        def _():
            act(relay(source, 0, k_up.at[d], above))

        for e in range(1, inner):
            act(relay(source, 0, k_in.at[d, e], o * inner + (c + e) % inner))
        for e in range(inner):
            slab = (o - d) * inner + (c + inner - e) % inner
            if start:
                arrived(slab, 1)

            @pl.when(o < outer - 1)
            def _(slab=slab, e=e):
                act(relay(slab, 1, v_up.at[d, e], above))

    own_plane(lambda copy: copy.start())

    def mask_rows(h, _):
        def filled(shape, value):
            return jnp.full(shape, value, jnp.int32)

        def on_slash(gap):
            hit = gap == slash_ref[h, 0]
            for i in range(1, slash_ref.shape[1]):
                hit = hit | (gap == slash_ref[h, i])
            return hit

        shape = (2 * slab_blocks, rows)
        row = lax.broadcasted_iota(jnp.int32, shape, 0)
        query_block = first_block + lax.broadcasted_iota(jnp.int32, shape, 1) // BLK
        block = first_block + jnp.where(row < slab_blocks, row, row - 2 * slab_blocks)
        gap = query_block - block

        def look(i, chosen):
            return jnp.where(block == vert_ref[h, i], 1, chosen)

        chosen = lax.fori_loop(0, chosen_count, look, filled(shape, 0))
        near = (gap == 0) | ((chosen > 0) & (gap > 0) & (row < slab_blocks))
        bias_ref[h, :2 * slab_blocks] = jnp.where(near | on_slash(gap), 0.0, NEGATIVE)

        shape = (n * CAP, rows)
        row = lax.broadcasted_iota(jnp.int32, shape, 0)
        query_block = first_block + lax.broadcasted_iota(jnp.int32, shape, 1) // BLK

        def extremes(i, found):
            low, high = found
            block = vert_ref[h, i]
            held = row // CAP == block // slab_blocks
            return (jnp.where(held, jnp.minimum(low, block), low),
                    jnp.where(held, jnp.maximum(high, block), high))

        low, high = lax.fori_loop(0, chosen_count, extremes, (filled(shape, none), filled(shape, -1)))
        block = jnp.where(row % CAP == 0, low, jnp.where(high > low, high, none))
        gap = query_block - block
        usable = jnp.where(on_slash(gap), 0, jnp.where(gap > 0, 1, 0))
        bias_ref[h, 2 * slab_blocks:] = jnp.where(usable > 0, 0.0, NEGATIVE)
        return 0

    lax.fori_loop(0, kv, mask_rows, 0)

    def attend(get_k, get_v, bias_row, causal):
        def one_head(h, _):
            k = get_k(h)
            vt = get_v(h).T
            pieces = k.shape[0] // BLK
            heads = [h * per_group + g for g in range(per_group)]
            rows_bias = [bias_ref[h, pl.ds(bias_row + i, 1), :] for i in range(pieces)]
            before = [None if causal else (top[j], total[j]) for j in heads]
            scores = []
            for j in heads:
                q = q_ref[:, pl.ds(pl.multiple_of(j * HEAD_DIM, HEAD_DIM), HEAD_DIM)]
                scores.append(lax.dot_general(k, q, (((1,), (1,)), ((), ())),
                                              preferred_element_type=jnp.float32))
            done = []
            for s, old in zip(scores, before):
                s = s * SCALE
                s = jnp.concatenate(
                    [s[i * BLK:(i + 1) * BLK] + rows_bias[i] for i in range(pieces)], axis=0)
                if causal:
                    keys_at = lax.broadcasted_iota(jnp.int32, s.shape, 0)
                    query_at = lax.broadcasted_iota(jnp.int32, s.shape, 1)
                    s = jnp.where(keys_at <= query_at, s, NEGATIVE)
                peak = jnp.max(s, axis=0, keepdims=True)
                shrink = None
                if not causal:
                    peak = jnp.maximum(old[0], peak)
                    shrink = jnp.exp2(old[0] - peak)
                p = jnp.exp2(s - peak)
                amount = jnp.sum(p, axis=0, keepdims=True)
                if not causal:
                    amount = old[1] * shrink + amount
                mix = jnp.dot(vt, p.astype(jnp.bfloat16), preferred_element_type=jnp.float32)
                done.append((peak, amount, shrink, mix))
            for j, (peak, amount, shrink, mix) in zip(heads, done):
                top[j] = peak
                total[j] = amount
                acc[j] = mix if causal else acc[j] * shrink + mix
            return 0

        lax.fori_loop(0, kv, one_head, 0)

    def lanes(h):
        return pl.ds(pl.multiple_of(h * HEAD_DIM, HEAD_DIM), HEAD_DIM)

    def attend_slots(slab, count):
        def get(first):
            return lambda h: jnp.concatenate(
                [slots[slab + i, first:first + slot_keys, lanes(h)] for i in range(count)], axis=0)

        attend(get(0), get(slot_keys), 2 * slab_blocks + slab * CAP, False)

    attend(lambda h: k_ref[:, lanes(h)], lambda h: v_ref[:, lanes(h)], 0, True)

    for e in range(1, inner):
        peer = (c + inner - e) % inner
        slab = o * inner + peer

        @pl.when((o < outer - 1) | (peer < c))
        def _(slab=slab):
            arrived(slab, 1)

        @pl.when(o < outer - 1)
        def _(slab=slab, e=e):
            relay(slab, 1, v_up.at[0, e], above).start()

    @pl.when(o > 0)
    def _():
        spread_plane(1, True)

    for near in range(inner - 1):
        @pl.when(near < c)
        def _(near=near):
            arrived(o * inner + near, 0)
            attend_slots(o * inner + near, 1)

    @pl.when(me > 0)
    def _():
        for i in range(2):
            remote(prev.at[i], prev.at[i], prev_send.at[i], prev_recv.at[i], above).wait_recv()
        attend(lambda h: prev[0, :, lanes(h)], lambda h: prev[1, :, lanes(h)], slab_blocks, False)

    step = 2 if inner % 2 == 0 else 1

    def plane(d, _):
        @pl.when(d < o)
        def _():
            spread_plane(d + 1, True)

        base = (o - d) * inner
        for part in range(0, inner, step):
            for i in range(part, part + step):
                @pl.when(c != i)
                def _(i=i):
                    arrived(base + i, 0)

            attend_slots(base + part, step)
        return 0

    lax.fori_loop(1, o + 1, plane, 0)

    def finish(j, _):
        a = acc[j] / total[j]
        attn[:, lanes(j)] = a.T.astype(jnp.bfloat16)
        return 0

    lax.fori_loop(0, kv * per_group, finish, 0)
    weight_copy.wait()
    tiles = give.shape[0]
    mine = pl.ds(pl.multiple_of(core * half, half), half)
    theirs = pl.ds(pl.multiple_of(other * half, half), half)

    def swap(t):
        return pltpu.make_async_remote_copy(
            src_ref=give.at[t], dst_ref=take.at[t], send_sem=x_send.at[t], recv_sem=x_recv.at[t],
            device_id=(me, other), device_id_type=MESH,
        )

    def project(t, _):
        columns = pl.ds(pl.multiple_of(t * tile, tile), tile)
        res[t] = jnp.dot(attn[...], w_ref[:, columns], preferred_element_type=jnp.float32)
        give[t] = res[t, theirs, :].astype(jnp.bfloat16)
        swap(t).start()
        return 0

    lax.fori_loop(0, tiles, project, 0)

    def add_up(t, _):
        columns = pl.ds(pl.multiple_of(t * tile, tile), tile)
        swap(t).wait_recv()
        out_ref[:, columns] = (res[t, mine, :] + take[t].astype(jnp.float32)).astype(out_ref.dtype)
        return 0

    lax.fori_loop(0, tiles, add_up, 0)

    def sent(t, _):
        swap(t).wait_send()
        return 0

    lax.fori_loop(0, tiles, sent, 0)
    own_plane(lambda copy: copy.wait_send())
    for e in range(1, inner):
        @pl.when(o < outer - 1)
        def _(e=e):
            relay(o * inner + (c + inner - e) % inner, 1, v_up.at[0, e], above).wait_send()

    def left(d, _):
        spread_plane(d, False)
        return 0

    lax.fori_loop(1, o + 1, left, 0)


def on_device(n, queries, keys, values, vertical, slash, out_weight):
    rows = queries.shape[0]
    kv = vertical.shape[0]
    per_group = queries.shape[1] // (kv * HEAD_DIM)
    slab_blocks = rows // BLK
    inner = math.gcd(n, 4)
    outer = n // inner
    model = out_weight.shape[1]
    cut = CAP * BLK + CAP * BLK // 2

    tile = math.gcd(model, 512)
    tiles = model // tile
    heads = kv * per_group
    vmem = pl.BlockSpec(memory_space=pltpu.VMEM)
    smem = pl.BlockSpec(memory_space=pltpu.SMEM)
    dma = pltpu.SemaphoreType.DMA
    return pl.pallas_call(
        functools.partial(kernel, n, inner, cut, kv, per_group, tile),
        out_shape=jax.ShapeDtypeStruct((rows // 2, model), jnp.bfloat16),
        in_specs=[vmem] * 3 + [smem] * 2 + [pl.BlockSpec(memory_space=pl.ANY)],
        out_specs=vmem,
        scratch_shapes=[
            pltpu.VMEM((2 * CAP * BLK, kv * HEAD_DIM), jnp.bfloat16),
            pltpu.VMEM((kv, 2 * slab_blocks + n * CAP, rows), jnp.float32),
            pltpu.VMEM((n, 2 * CAP * BLK, kv * HEAD_DIM), jnp.bfloat16),
            pltpu.VMEM((2, rows, kv * HEAD_DIM), jnp.bfloat16),
            pltpu.VMEM(out_weight.shape, jnp.bfloat16),
            pltpu.VMEM((heads, HEAD_DIM, rows), jnp.float32),
            pltpu.VMEM((heads, 1, rows), jnp.float32),
            pltpu.VMEM((heads, 1, rows), jnp.float32),
            pltpu.VMEM((rows, heads * HEAD_DIM), jnp.bfloat16),
            pltpu.VMEM((tiles, rows, tile), jnp.float32),
            pltpu.VMEM((tiles, rows // 2, tile), jnp.bfloat16),
            pltpu.VMEM((tiles, rows // 2, tile), jnp.bfloat16),
            dma,
            dma((2,)),
            dma((2,)),
            dma((n, 2)),
            dma((outer,)),
            dma((outer, inner)),
            dma((inner,)),
            dma((outer, inner)),
            dma((tiles,)),
            dma((tiles,)),
        ],
        compiler_params=pltpu.CompilerParams(
            collective_id=0, has_side_effects=True, vmem_limit_bytes=60 * 2**20
        ),
    )(queries, keys, values, vertical, slash, out_weight)


def solution(mesh):
    placed = (
        P("seq", "head"),
        P("seq", "head"),
        P("seq", "head"),
        P("head", None),
        P("head", None),
        P("head", None),
    )
    return jax.shard_map(
        functools.partial(on_device, mesh.shape["seq"]),
        mesh=mesh, in_specs=placed, out_specs=P(("seq", "head"), None), check_vma=False,
    )
```

profile of v0, /device:TPU:103, one launch (start us, length us, event | category | flops | bytes accessed | tf_op | source)
XLA Modules:
  0.0 191.3 jit_solution(6249234179410017272)
XLA Ops:
  0.0 1.3 copy.7.slash_ref
  1.3 187.6 %shard_map.64 = bf16[128,4096]{1,0:T(8,128)(2,1)} custom-call(bf16[256,2048]{1,0:T(8,128)(2,1)} %q_ref.1, bf16[256,512]{1,0:T(8,128)(2,1)} %k_ref.1, bf16[256,512]{1,0:T(8,128)(2,1)} %v_ref.1, s32[4,64]{1,0:T(4,128)} %vert_ref.1, s32[4,2]{1,0:T(4,128)} %copy.7.slash_ref, bf16[2048,4096]{1,0:T(8,128)(2,1)} %w_hbm.1), custom_call_target="tpu_custom_call" | custom-call | tf_op jit(solution)/shard_map/pallas_call | solution.py:360
  189.0 2.3 %copy.9 = bf16[128,4096]{1,0:T(8,128)(2,1)} copy(bf16[128,4096]{1,0:T(8,128)(2,1)} %shard_map.64) | data formatting | bytes 2097152
where the time goes:
time: 191 us
  Pallas kernels  188 us (98%)
  local copies, waits for them, and re-layouts  3.62 us (2%)
    pallas_call x1, Pallas kernels, on_device(): pl.pallas_call(functools.partial(kernel, n, inner, cut, kv, per_group, ti...  188 us

commit v1 on v0

v1 whole, which is shorter than its diff:
```python
import functools
import math

import jax
import jax.numpy as jnp
from jax import lax
from jax.experimental import pallas as pl
from jax.experimental.pallas import tpu as pltpu
from jax.sharding import PartitionSpec as P

HEAD_DIM = 128
BLK = 64
CAP = 2
NEGATIVE = -1e30
MESH = pl.DeviceIdType.MESH
SCALE = HEAD_DIM ** (-0.5) * math.log2(math.e)
SIDE = 4
FAR_CHUNK = 8


def kernel(
    per_group, tile,
    q_ref, k_ref, v_ref, vert_ref, slash_ref, w_hbm, out_ref,
    pack, slots, qg, kg, vg, kc, vtc, w_ref, acc, top, total, o_buf, attn, res, give, take,
    w_sem, pack_send, kv_send, kv_recv, q_send, q_recv, slot_recv, ring_send,
    o_send, o_recv, x_send, x_recv,
):
    rows = q_ref.shape[0]
    me = lax.axis_index("seq")
    core = lax.axis_index("head")
    other = 1 - core
    o, c = me // SIDE, me % SIDE
    x, z = o // SIDE, o % SIDE
    slab_blocks = rows // BLK
    half = rows // 2
    width = per_group * HEAD_DIM
    chosen_count = vert_ref.shape[1]
    next_plane = (me + SIDE) % (SIDE ** 3)
    last_plane = (me + SIDE ** 3 - SIDE) % (SIDE ** 3)

    def at(xx, zz, cc):
        return (xx % SIDE * SIDE + zz % SIDE) * SIDE + cc

    barrier = pltpu.get_barrier_semaphore()

    def greet(seq, head):
        pl.semaphore_signal(barrier, inc=1, device_id=(seq, head), device_id_type=MESH)

    greet(me, other)
    for d in range(1, SIDE):
        greet(o * SIDE + (c + d) % SIDE, core)
    for step in (1, SIDE - 1):
        greet(at(x + step, z, c), core)
        greet(at(x, z + step, c), core)
    greet(next_plane, core)
    greet(last_plane, core)

    weight_copy = pltpu.make_async_copy(w_hbm, w_ref, w_sem)
    weight_copy.start()

    def lanes(h, size=HEAD_DIM):
        return pl.ds(pl.multiple_of(h * size, size), size)

    first_block = me * slab_blocks
    for h in range(SIDE):
        low, high = jnp.int32(slab_blocks), jnp.int32(-1)
        for e in range(chosen_count):
            block = vert_ref[h, e] - first_block
            inside = (block >= 0) & (block < slab_blocks)
            low = jnp.where(inside, jnp.minimum(low, block), low)
            high = jnp.where(inside, jnp.maximum(high, block), high)
        for slot, block in enumerate((low, high)):
            for part, source in enumerate((k_ref, v_ref)):
                got = source[:BLK, h * HEAD_DIM:(h + 1) * HEAD_DIM]
                for i in range(1, slab_blocks):
                    rows_i = source[i * BLK:(i + 1) * BLK, h * HEAD_DIM:(h + 1) * HEAD_DIM]
                    got = jnp.where(block == i, rows_i, got)
                pack[h, part * CAP + slot] = got
    for i in range(2 * CAP):
        slots[me * (2 * CAP) + i] = pack[c, i]
    kg[c + 1] = k_ref[:, lanes(c)]
    vg[c + 1] = v_ref[:, lanes(c)]
    qg[c] = q_ref[:, lanes(c, width)]

    pl.semaphore_wait(barrier, 1 + (SIDE - 1) + 4 + 2)

    def remote(src, dst, send_sem, recv_sem, seq):
        return pltpu.make_async_remote_copy(
            src_ref=src, dst_ref=dst, send_sem=send_sem, recv_sem=recv_sem,
            device_id=(seq, core), device_id_type=MESH,
        )

    def held(slab):
        return slots.at[pl.ds(slab * (2 * CAP), 2 * CAP)]

    def peer(d):
        return (c + d) % SIDE

    def pack_copy(d):
        return remote(pack.at[peer(d)], held(me), pack_send.at[d], slot_recv.at[me], o * SIDE + peer(d))

    def kv_copies(d):
        to = peer(d)
        return [
            remote(source.at[:, lanes(to)], got.at[c + 1], kv_send.at[d, i], kv_recv.at[c + 1, i], o * SIDE + to)
            for i, (source, got) in enumerate(((k_ref, kg), (v_ref, vg)))
        ]

    def q_copy(d):
        to = peer(d)
        return remote(q_ref.at[:, lanes(to, width)], qg.at[c], q_send.at[d], q_recv.at[c], o * SIDE + to)

    def next_copies():
        return [
            remote(got.at[SIDE], got.at[0], kv_send.at[0, i], kv_recv.at[0, i], next_plane)
            for i, got in enumerate((kg, vg))
        ]

    near_order = (1, SIDE - 1, 2)
    for d in near_order:
        pack_copy(d).start()
    for d in near_order:
        for copy in kv_copies(d):
            copy.start()
    for d in near_order:
        q_copy(d).start()

    def slab_of(dp, dq, kind):
        dx, dz = (dp, dq) if kind < 2 else (dq, dp)
        return at(x + SIDE - dx, z + SIDE - dz, kind)

    def ring(slab, kind, phase, sign):
        along_x = (kind < 2) == (phase == 0)
        to = at(x + SIDE + sign, z, c) if along_x else at(x, z + SIDE + sign, c)
        there = held(slab)
        way = (0 if along_x else 2) + (sign > 0)
        return remote(there, there, ring_send.at[slab, way], slot_recv.at[slab], to)

    def arrived(slab):
        there = held(slab)
        remote(there, there, ring_send.at[slab, 0], slot_recv.at[slab], next_plane).wait_recv()

    def sign_of(kind):
        return 1 if kind % 2 == 0 else -1

    def own(act):
        for kind in range(SIDE):
            slab = slab_of(0, 0, kind)
            act(slab, kind, [(0, 1), (0, -1), (1, 1), (1, -1)])

    def first(dp, act):
        for kind in range(SIDE):
            ways = [(0, dp)] if dp == sign_of(kind) else []
            act(slab_of(dp, 0, kind), kind, ways + [(1, 1), (1, -1)])

    def second(dp, dq, act):
        for kind in range(SIDE):
            act(slab_of(dp, dq, kind), kind, [(1, dq)] if dq == sign_of(kind) else [])

    def pass_on(slab, kind, ways):
        arrived(slab)
        for phase, sign in ways:
            ring(slab, kind, phase, sign).start()

    def pass_own(slab, kind, ways):
        @pl.when(c != kind)
        def _():
            arrived(slab)

        for phase, sign in ways:
            ring(slab, kind, phase, sign).start()

    def sent(slab, kind, ways):
        for phase, sign in ways:
            ring(slab, kind, phase, sign).wait_send()

    own(pass_own)
    for dp in (1, -1, 2):
        first(dp, pass_on)

    for d in range(1, SIDE):
        for i, got in enumerate((kg, vg)):
            there = got.at[peer(d) + 1]
            remote(there, there, kv_send.at[d, i], kv_recv.at[peer(d) + 1, i], next_plane).wait_recv()
    for copy in next_copies():
        copy.start()
    for copy in next_copies():
        copy.wait_recv()

    heads = range(per_group)

    def near(i):
        base = (o * SIDE + i) * slab_blocks
        k = jnp.concatenate([kg[i], kg[i + 1]], axis=0)
        vt = jnp.concatenate([vg[i], vg[i + 1]], axis=0).T
        shape = (2 * slab_blocks, rows)
        block = lax.broadcasted_iota(jnp.int32, shape, 0) - slab_blocks
        gap = lax.broadcasted_iota(jnp.int32, shape, 1) // BLK - block
        block = base + block
        good = gap == 0
        for j in range(slash_ref.shape[1]):
            good = good | (gap == slash_ref[c, j])
        chosen = block == vert_ref[c, 0]
        for e in range(1, chosen_count):
            chosen = chosen | (block == vert_ref[c, e])
        good = good | (chosen & (gap > 0))
        bias = jnp.where(good & (block >= 0), 0.0, NEGATIVE)
        keys_at = lax.broadcasted_iota(jnp.int32, (rows, rows), 0)
        query_at = lax.broadcasted_iota(jnp.int32, (rows, rows), 1)
        causal = keys_at <= query_at
        scores = []
        for g in heads:
            q = qg[i, :, g * HEAD_DIM:(g + 1) * HEAD_DIM]
            scores.append(lax.dot_general(k, q, (((1,), (1,)), ((), ())), preferred_element_type=jnp.float32))
        for g, s in zip(heads, scores):
            s = s * SCALE
            s = jnp.concatenate(
                [s[j * BLK:(j + 1) * BLK] + bias[j:j + 1] for j in range(2 * slab_blocks)], axis=0)
            s = jnp.concatenate([s[:rows], jnp.where(causal, s[rows:], NEGATIVE)], axis=0)
            peak = jnp.max(s, axis=0, keepdims=True)
            p = jnp.exp2(s - peak)
            top[i, g] = peak
            total[i, g] = jnp.sum(p, axis=0, keepdims=True)
            acc[i, g] = jnp.dot(vt, p.astype(jnp.bfloat16), preferred_element_type=jnp.float32)

    def near_and_pass(step, _):
        i = (c + step) % SIDE

        @pl.when(step > 0)
        def _():
            remote(qg.at[i], qg.at[i], q_send.at[1], q_recv.at[i], next_plane).wait_recv()

        for dq in (1, -1):
            second(step, dq, pass_on)
        near(i)
        return 0

    lax.fori_loop(0, SIDE, near_and_pass, 0)

    def last_ones(step, _):
        second(step, 2, lambda slab, kind, ways: arrived(slab))
        return 0

    lax.fori_loop(0, SIDE, last_ones, 0)

    limit = (o * SIDE + lax.broadcasted_iota(jnp.int32, (BLK, HEAD_DIM), 1) - 1) * slab_blocks
    chunks = jnp.minimum(chosen_count // FAR_CHUNK, o + 1)

    def collect(pair, _):
        got = []
        for j in range(2):
            e = pair * 2 + j
            slab = vert_ref[c, e] // slab_blocks
            before = jnp.where(e > 0, vert_ref[c, jnp.maximum(e - 1, 0)] // slab_blocks, -1)
            place = slab * (2 * CAP) + jnp.where(before == slab, 1, 0)
            at_row = pl.ds(pl.multiple_of(e * BLK, BLK), BLK)
            kc[at_row, :HEAD_DIM] = slots[place]
            kc[at_row, HEAD_DIM:] = jnp.where(vert_ref[c, e] < limit, 0.0, NEGATIVE).astype(jnp.bfloat16)
            got.append(slots[place + CAP])
        vtc[pair] = jnp.concatenate(got, axis=0).T
        return 0

    lax.fori_loop(0, chunks * (FAR_CHUNK // 2), collect, 0)

    def o_copy(i, to):
        return remote(o_buf.at[i], attn.at[c], o_send.at[i], o_recv.at[c], o * SIDE + to)

    def far_slab(step, _):
        i = (c + SIDE - 1 - step) % SIDE
        mark = (lax.broadcasted_iota(jnp.int32, (rows, HEAD_DIM), 1) == i).astype(jnp.bfloat16)

        def chunk(n, _):
            k = kc[pl.ds(pl.multiple_of(n * FAR_CHUNK * BLK, FAR_CHUNK * BLK), FAR_CHUNK * BLK), :]
            vt = jnp.concatenate([vtc[n * (FAR_CHUNK // 2) + j] for j in range(FAR_CHUNK // 2)], axis=1)
            scores = []
            old = [(top[i, g], total[i, g]) for g in heads]
            for g in heads:
                q = jnp.concatenate([qg[i, :, g * HEAD_DIM:(g + 1) * HEAD_DIM], mark], axis=1)
                scores.append(lax.dot_general(k, q, (((1,), (1,)), ((), ())), preferred_element_type=jnp.float32))
            done = []
            for s, (peak_old, amount_old) in zip(scores, old):
                s = s * SCALE
                peak = jnp.maximum(peak_old, jnp.max(s, axis=0, keepdims=True))
                shrink = jnp.exp2(peak_old - peak)
                p = jnp.exp2(s - peak)
                amount = amount_old * shrink + jnp.sum(p, axis=0, keepdims=True)
                mix = jnp.dot(vt, p.astype(jnp.bfloat16), preferred_element_type=jnp.float32)
                done.append((peak, amount, shrink, mix))
            for g, (peak, amount, shrink, mix) in zip(heads, done):
                top[i, g] = peak
                total[i, g] = amount
                acc[i, g] = acc[i, g] * shrink + mix
            return 0

        lax.fori_loop(0, chunks, chunk, 0)
        for g in heads:
            a = acc[i, g] * (1.0 / total[i, g])
            o_buf[i, :, g * HEAD_DIM:(g + 1) * HEAD_DIM] = a.T.astype(jnp.bfloat16)

        @pl.when(step < SIDE - 1)
        def _():
            o_copy(i, i).start()

        return 0

    lax.fori_loop(0, SIDE, far_slab, 0)
    attn[c] = o_buf[c]
    for d in range(1, SIDE):
        there = attn.at[peer(d)]
        remote(there, there, o_send.at[peer(d)], o_recv.at[peer(d)], next_plane).wait_recv()

    weight_copy.wait()
    tiles = give.shape[0]
    mine = pl.ds(pl.multiple_of(core * half, half), half)
    theirs = pl.ds(pl.multiple_of(other * half, half), half)

    def swap(t):
        return pltpu.make_async_remote_copy(
            src_ref=give.at[t], dst_ref=take.at[t], send_sem=x_send.at[t], recv_sem=x_recv.at[t],
            device_id=(me, other), device_id_type=MESH,
        )

    def project(t, _):
        columns = pl.ds(pl.multiple_of(t * tile, tile), tile)
        a = jnp.concatenate([attn[j] for j in range(SIDE)], axis=1)
        res[t] = jnp.dot(a, w_ref[:, columns], preferred_element_type=jnp.float32)
        give[t] = res[t, theirs, :].astype(jnp.bfloat16)
        swap(t).start()
        return 0

    lax.fori_loop(0, tiles, project, 0)

    def add_up(t, _):
        columns = pl.ds(pl.multiple_of(t * tile, tile), tile)
        swap(t).wait_recv()
        out_ref[:, columns] = (res[t, mine, :] + take[t].astype(jnp.float32)).astype(out_ref.dtype)
        return 0

    lax.fori_loop(0, tiles, add_up, 0)

    def swapped(t, _):
        swap(t).wait_send()
        return 0

    lax.fori_loop(0, tiles, swapped, 0)
    for d in range(1, SIDE):
        pack_copy(d).wait_send()
        for copy in kv_copies(d):
            copy.wait_send()
        q_copy(d).wait_send()
        o_copy(peer(d), peer(d)).wait_send()
    for copy in next_copies():
        copy.wait_send()
    own(sent)
    for dp in (1, -1, 2):
        first(dp, sent)

    def ring_sent(step, _):
        for dq in (1, -1):
            second(step, dq, sent)
        return 0

    lax.fori_loop(0, SIDE, ring_sent, 0)


def on_device(n, queries, keys, values, vertical, slash, out_weight):
    rows = queries.shape[0]
    kv = vertical.shape[0]
    per_group = queries.shape[1] // (kv * HEAD_DIM)
    width = per_group * HEAD_DIM
    model = out_weight.shape[1]
    listed = vertical.shape[1]

    tile = math.gcd(model, 512)
    tiles = model // tile
    vmem = pl.BlockSpec(memory_space=pltpu.VMEM)
    smem = pl.BlockSpec(memory_space=pltpu.SMEM)
    dma = pltpu.SemaphoreType.DMA
    return pl.pallas_call(
        functools.partial(kernel, per_group, tile),
        out_shape=jax.ShapeDtypeStruct((rows // 2, model), jnp.bfloat16),
        in_specs=[vmem] * 3 + [smem] * 2 + [pl.BlockSpec(memory_space=pl.ANY)],
        out_specs=vmem,
        scratch_shapes=[
            pltpu.VMEM((kv, 2 * CAP, BLK, HEAD_DIM), jnp.bfloat16),
            pltpu.VMEM((n * 2 * CAP, BLK, HEAD_DIM), jnp.bfloat16),
            pltpu.VMEM((SIDE, rows, width), jnp.bfloat16),
            pltpu.VMEM((SIDE + 1, rows, HEAD_DIM), jnp.bfloat16),
            pltpu.VMEM((SIDE + 1, rows, HEAD_DIM), jnp.bfloat16),
            pltpu.VMEM((listed * BLK, 2 * HEAD_DIM), jnp.bfloat16),
            pltpu.VMEM((listed // 2, HEAD_DIM, 2 * BLK), jnp.bfloat16),
            pltpu.VMEM(out_weight.shape, jnp.bfloat16),
            pltpu.VMEM((SIDE, per_group, HEAD_DIM, rows), jnp.float32),
            pltpu.VMEM((SIDE, per_group, 1, rows), jnp.float32),
            pltpu.VMEM((SIDE, per_group, 1, rows), jnp.float32),
            pltpu.VMEM((SIDE, rows, width), jnp.bfloat16),
            pltpu.VMEM((SIDE, rows, width), jnp.bfloat16),
            pltpu.VMEM((tiles, rows, tile), jnp.float32),
            pltpu.VMEM((tiles, rows // 2, tile), jnp.bfloat16),
            pltpu.VMEM((tiles, rows // 2, tile), jnp.bfloat16),
            dma,
            dma((SIDE,)),
            dma((SIDE, 2)),
            dma((SIDE + 1, 2)),
            dma((SIDE,)),
            dma((SIDE,)),
            dma((n,)),
            dma((n, SIDE)),
            dma((SIDE,)),
            dma((SIDE,)),
            dma((tiles,)),
            dma((tiles,)),
        ],
        compiler_params=pltpu.CompilerParams(
            collective_id=0, has_side_effects=True, vmem_limit_bytes=60 * 2**20
        ),
    )(queries, keys, values, vertical, slash, out_weight)


def solution(mesh):
    placed = (
        P("seq", "head"),
        P("seq", "head"),
        P("seq", "head"),
        P("head", None),
        P("head", None),
        P("head", None),
    )
    return jax.shard_map(
        functools.partial(on_device, mesh.shape["seq"]),
        mesh=mesh, in_specs=placed, out_specs=P(("seq", "head"), None), check_vma=False,
    )
```

time: 191 us -> 93.2 us (0.49)
  the two profiles are of different devices: /device:TPU:103 before, /device:TPU:7 now
where the time goes in v1:
time: 93.2 us; the launch traced here: 92.9 us
  Pallas kernels  89.2 us (96%)
  local copies, waits for them, and re-layouts  3.62 us (4%)
    pallas_call x1, Pallas kernels, on_device(): pl.pallas_call(functools.partial(kernel, per_group, tile), out_shape=jax....  89.2 us
    unnamed x2, local copies, waits for them, and re-layouts  3.62 us

profile of v1, /device:TPU:7, one launch (start us, length us, event | category | flops | bytes accessed | tf_op | source)
XLA Modules:
  0.0 92.9 jit_solution(11280360459482198631)
XLA Ops:
  0.0 1.3 %copy.7.slash_ref = s32[4,2]{1,0:T(4,128)} copy(s32[4,2]{0,1:T(2,128)} %param.10) | data formatting | bytes 64 | tf_op args[4]
  1.3 89.2 %shard_map.64 = bf16[128,4096]{1,0:T(8,128)(2,1)} custom-call(bf16[256,2048]{1,0:T(8,128)(2,1)} %q_ref.1, bf16[256,512]{1,0:T(8,128)(2,1)} %k_ref.1, bf16[256,512]{1,0:T(8,128)(2,1)} %v_ref.1, s32[4,64]{1,0:T(4,128)} %vert_ref.1, s32[4,2]{1,0:T(4,128)} %copy.7.slash_ref, bf16[2048,4096]{1,0:T(8,128)(2,1)} %w_hbm.1), custom_call_target="tpu_custom_call" | custom-call | tf_op jit(solution)/shard_map/pallas_call | solution.py:379
  90.6 2.3 %copy.9 = bf16[128,4096]{1,0:T(8,128)(2,1)} copy(bf16[128,4096]{1,0:T(8,128)(2,1)} %shard_map.64) | data formatting | bytes 2097152

commit v2 on v1

--- a/solution.py
+++ b/solution.py
@@ -15,13 +15,14 @@
 MESH = pl.DeviceIdType.MESH
 SCALE = HEAD_DIM ** (-0.5) * math.log2(math.e)
 SIDE = 4
-FAR_CHUNK = 8
+FAR_CHUNK = 16
+AUX = 16
 
 
 def kernel(
     per_group, tile,
     q_ref, k_ref, v_ref, vert_ref, slash_ref, w_hbm, out_ref,
-    pack, slots, qg, kg, vg, kc, vtc, w_ref, acc, top, total, o_buf, attn, res, give, take,
+    packs, slots, qg, qt, kg, vg, kc, vtc, w_ref, acc, top, total, o_buf, attn, res, give, take,
     w_sem, pack_send, kv_send, kv_recv, q_send, q_recv, slot_recv, ring_send,
     o_send, o_recv, x_send, x_recv,
 ):
@@ -75,9 +76,10 @@
                 for i in range(1, slab_blocks):
                     rows_i = source[i * BLK:(i + 1) * BLK, h * HEAD_DIM:(h + 1) * HEAD_DIM]
                     got = jnp.where(block == i, rows_i, got)
-                pack[h, part * CAP + slot] = got
-    for i in range(2 * CAP):
-        slots[me * (2 * CAP) + i] = pack[c, i]
+                packs[part][h, slot] = got
+    for part in range(2):
+        for i in range(CAP):
+            slots[part][me * CAP + i] = packs[part][c, i]
     kg[c + 1] = k_ref[:, lanes(c)]
     vg[c + 1] = v_ref[:, lanes(c)]
     qg[c] = q_ref[:, lanes(c, width)]
@@ -90,14 +92,15 @@
             device_id=(seq, core), device_id_type=MESH,
         )
 
-    def held(slab):
-        return slots.at[pl.ds(slab * (2 * CAP), 2 * CAP)]
+    def held(part, slab):
+        return slots[part].at[pl.ds(slab * CAP, CAP)]
 
     def peer(d):
         return (c + d) % SIDE
 
-    def pack_copy(d):
-        return remote(pack.at[peer(d)], held(me), pack_send.at[d], slot_recv.at[me], o * SIDE + peer(d))
+    def pack_copy(part, d):
+        return remote(packs[part].at[peer(d)], held(part, me), pack_send.at[part, d], slot_recv.at[part, me],
+                      o * SIDE + peer(d))
 
     def kv_copies(d):
         to = peer(d)
@@ -117,8 +120,9 @@
         ]
 
     near_order = (1, SIDE - 1, 2)
-    for d in near_order:
-        pack_copy(d).start()
+    for part in range(2):
+        for d in near_order:
+            pack_copy(part, d).start()
     for d in near_order:
         for copy in kv_copies(d):
             copy.start()
@@ -129,16 +133,16 @@
         dx, dz = (dp, dq) if kind < 2 else (dq, dp)
         return at(x + SIDE - dx, z + SIDE - dz, kind)
 
-    def ring(slab, kind, phase, sign):
+    def ring(part, slab, kind, phase, sign):
         along_x = (kind < 2) == (phase == 0)
         to = at(x + SIDE + sign, z, c) if along_x else at(x, z + SIDE + sign, c)
-        there = held(slab)
+        there = held(part, slab)
         way = (0 if along_x else 2) + (sign > 0)
-        return remote(there, there, ring_send.at[slab, way], slot_recv.at[slab], to)
-
-    def arrived(slab):
-        there = held(slab)
-        remote(there, there, ring_send.at[slab, 0], slot_recv.at[slab], next_plane).wait_recv()
+        return remote(there, there, ring_send.at[part, slab, way], slot_recv.at[part, slab], to)
+
+    def arrived(part, slab):
+        there = held(part, slab)
+        remote(there, there, pack_send.at[part, 1], slot_recv.at[part, slab], next_plane).wait_recv()
 
     def sign_of(kind):
         return 1 if kind % 2 == 0 else -1
@@ -157,26 +161,36 @@
         for kind in range(SIDE):
             act(slab_of(dp, dq, kind), kind, [(1, dq)] if dq == sign_of(kind) else [])
 
-    def pass_on(slab, kind, ways):
-        arrived(slab)
-        for phase, sign in ways:
-            ring(slab, kind, phase, sign).start()
-
-    def pass_own(slab, kind, ways):
-        @pl.when(c != kind)
-        def _():
-            arrived(slab)
-
-        for phase, sign in ways:
-            ring(slab, kind, phase, sign).start()
-
-    def sent(slab, kind, ways):
-        for phase, sign in ways:
-            ring(slab, kind, phase, sign).wait_send()
-
-    own(pass_own)
+    def pass_on(part):
+        def act(slab, kind, ways):
+            arrived(part, slab)
+            for phase, sign in ways:
+                ring(part, slab, kind, phase, sign).start()
+
+        return act
+
+    def pass_own(part):
+        def act(slab, kind, ways):
+            @pl.when(c != kind)
+            def _():
+                arrived(part, slab)
+
+            for phase, sign in ways:
+                ring(part, slab, kind, phase, sign).start()
+
+        return act
+
+    def sent(part):
+        def act(slab, kind, ways):
+            for phase, sign in ways:
+                ring(part, slab, kind, phase, sign).wait_send()
+
+        return act
+
+    own(pass_own(0))
     for dp in (1, -1, 2):
-        first(dp, pass_on)
+        first(dp, pass_on(0))
+    own(pass_own(1))
 
     for d in range(1, SIDE):
         for i, got in enumerate((kg, vg)):
@@ -184,10 +198,14 @@
             remote(there, there, kv_send.at[d, i], kv_recv.at[peer(d) + 1, i], next_plane).wait_recv()
     for copy in next_copies():
         copy.start()
-    for copy in next_copies():
-        copy.wait_recv()
 
     heads = range(per_group)
+
+    def turn(i):
+        row = lax.broadcasted_iota(jnp.int32, (HEAD_DIM, rows), 0)
+        for g in heads:
+            qt[i, g, :HEAD_DIM] = qg[i, :, g * HEAD_DIM:(g + 1) * HEAD_DIM].T
+            qt[i, g, HEAD_DIM:] = jnp.where(row == i, 1.0, 0.0).astype(jnp.bfloat16)
 
     def near(i):
         base = (o * SIDE + i) * slab_blocks
@@ -198,8 +216,8 @@
         gap = lax.broadcasted_iota(jnp.int32, shape, 1) // BLK - block
         block = base + block
         good = gap == 0
-        for j in range(slash_ref.shape[1]):
-            good = good | (gap == slash_ref[c, j])
+        for j in range(slash_ref.shape[0]):
+            good = good | (gap == slash_ref[j, c])
         chosen = block == vert_ref[c, 0]
         for e in range(1, chosen_count):
             chosen = chosen | (block == vert_ref[c, e])
@@ -210,86 +228,123 @@
         causal = keys_at <= query_at
         scores = []
         for g in heads:
-            q = qg[i, :, g * HEAD_DIM:(g + 1) * HEAD_DIM]
-            scores.append(lax.dot_general(k, q, (((1,), (1,)), ((), ())), preferred_element_type=jnp.float32))
+            scores.append(jnp.dot(k, qt[i, g, :HEAD_DIM], preferred_element_type=jnp.float32))
         for g, s in zip(heads, scores):
-            s = s * SCALE
             s = jnp.concatenate(
                 [s[j * BLK:(j + 1) * BLK] + bias[j:j + 1] for j in range(2 * slab_blocks)], axis=0)
             s = jnp.concatenate([s[:rows], jnp.where(causal, s[rows:], NEGATIVE)], axis=0)
             peak = jnp.max(s, axis=0, keepdims=True)
-            p = jnp.exp2(s - peak)
+            p = jnp.exp2((s - peak) * SCALE)
             top[i, g] = peak
             total[i, g] = jnp.sum(p, axis=0, keepdims=True)
             acc[i, g] = jnp.dot(vt, p.astype(jnp.bfloat16), preferred_element_type=jnp.float32)
 
-    def near_and_pass(step, _):
+    def second_keys(step, _):
+        for dq in (1, -1):
+            second(step, dq, pass_on(0))
+        return 0
+
+    def last_ones(part):
+        def one(step, _):
+            second(step, 2, lambda slab, kind, ways: arrived(part, slab))
+            return 0
+
+        lax.fori_loop(0, SIDE, one, 0)
+
+    lax.fori_loop(0, SIDE, second_keys, 0)
+    turn(c)
+    for dp in (1, -1, 2):
+        first(dp, pass_on(1))
+    for copy in next_copies():
+        copy.wait_recv()
+    last_ones(0)
+
+    lane = lax.broadcasted_iota(jnp.int32, (BLK, HEAD_DIM), 1)
+    limit = (o * SIDE + lane - 1) * slab_blocks
+    unit = jnp.where((lane >= SIDE) & (lane < SIDE + 3), 1.0, 0.0)
+    chunks = jnp.minimum(chosen_count // FAR_CHUNK, (o + 2) // 2)
+
+    def place(e):
+        slab = vert_ref[c, e] // slab_blocks
+        before = jnp.where(e > 0, vert_ref[c, jnp.maximum(e - 1, 0)] // slab_blocks, -1)
+        return slab * CAP + jnp.where(before == slab, 1, 0)
+
+    def collect_keys(n, _):
+        for j in range(8):
+            e = n * 8 + j
+            at_row = pl.ds(pl.multiple_of(e * BLK, BLK), BLK)
+            kc[at_row, :HEAD_DIM] = slots[0][place(e)]
+            mask = jnp.where((lane < SIDE) & (vert_ref[c, e] >= limit), NEGATIVE, unit)
+            kc[at_row, HEAD_DIM:] = mask.astype(jnp.bfloat16)
+        return 0
+
+    def collect_values(n, _):
+        for j in range(4):
+            pair = n * 4 + j
+            both = jnp.concatenate([slots[1][place(pair * 2)], slots[1][place(pair * 2 + 1)]], axis=0)
+            vtc[pair] = both.T
+        return 0
+
+    def keys_of(n):
+        return kc[pl.ds(pl.multiple_of(n * FAR_CHUNK * BLK, FAR_CHUNK * BLK), FAR_CHUNK * BLK), :]
+
+    def largest(i):
+        def chunk(n, peaks):
+            k = keys_of(n)
+            return tuple(
+                jnp.maximum(peak, jnp.max(jnp.dot(k, qt[i, g], preferred_element_type=jnp.float32),
+                                          axis=0, keepdims=True))
+                for g, peak in zip(heads, peaks))
+
+        near_peaks = tuple(top[i, g] for g in heads)
+        peaks = lax.fori_loop(0, chunks, chunk, near_peaks)
+        row = lax.broadcasted_iota(jnp.int32, (AUX, rows), 0)
+        for g, peak, old in zip(heads, peaks, near_peaks):
+            shrink = jnp.exp2((old - peak) * SCALE)
+            total[i, g] = total[i, g] * shrink
+            acc[i, g] = acc[i, g] * shrink
+            rest = -peak
+            aux = jnp.where(row == i, 1.0, 0.0)
+            for j in range(3):
+                part = rest.astype(jnp.bfloat16).astype(jnp.float32)
+                aux = jnp.where(row == SIDE + j, part, aux)
+                rest = rest - part
+            qt[i, g, HEAD_DIM:HEAD_DIM + AUX] = aux.astype(jnp.bfloat16)
+
+    lax.fori_loop(0, chunks * (FAR_CHUNK // 8), collect_keys, 0)
+
+    def first_pass(step, _):
         i = (c + step) % SIDE
 
         @pl.when(step > 0)
         def _():
             remote(qg.at[i], qg.at[i], q_send.at[1], q_recv.at[i], next_plane).wait_recv()
+            turn(i)
 
         for dq in (1, -1):
-            second(step, dq, pass_on)
+            second(step, dq, pass_on(1))
         near(i)
-        return 0
-
-    lax.fori_loop(0, SIDE, near_and_pass, 0)
-
-    def last_ones(step, _):
-        second(step, 2, lambda slab, kind, ways: arrived(slab))
-        return 0
-
-    lax.fori_loop(0, SIDE, last_ones, 0)
-
-    limit = (o * SIDE + lax.broadcasted_iota(jnp.int32, (BLK, HEAD_DIM), 1) - 1) * slab_blocks
-    chunks = jnp.minimum(chosen_count // FAR_CHUNK, o + 1)
-
-    def collect(pair, _):
-        got = []
-        for j in range(2):
-            e = pair * 2 + j
-            slab = vert_ref[c, e] // slab_blocks
-            before = jnp.where(e > 0, vert_ref[c, jnp.maximum(e - 1, 0)] // slab_blocks, -1)
-            place = slab * (2 * CAP) + jnp.where(before == slab, 1, 0)
-            at_row = pl.ds(pl.multiple_of(e * BLK, BLK), BLK)
-            kc[at_row, :HEAD_DIM] = slots[place]
-            kc[at_row, HEAD_DIM:] = jnp.where(vert_ref[c, e] < limit, 0.0, NEGATIVE).astype(jnp.bfloat16)
-            got.append(slots[place + CAP])
-        vtc[pair] = jnp.concatenate(got, axis=0).T
-        return 0
-
-    lax.fori_loop(0, chunks * (FAR_CHUNK // 2), collect, 0)
+        largest(i)
+        return 0
+
+    lax.fori_loop(0, SIDE, first_pass, 0)
+    last_ones(1)
+    lax.fori_loop(0, chunks * (FAR_CHUNK // 8), collect_values, 0)
 
     def o_copy(i, to):
         return remote(o_buf.at[i], attn.at[c], o_send.at[i], o_recv.at[c], o * SIDE + to)
 
     def far_slab(step, _):
         i = (c + SIDE - 1 - step) % SIDE
-        mark = (lax.broadcasted_iota(jnp.int32, (rows, HEAD_DIM), 1) == i).astype(jnp.bfloat16)
 
         def chunk(n, _):
-            k = kc[pl.ds(pl.multiple_of(n * FAR_CHUNK * BLK, FAR_CHUNK * BLK), FAR_CHUNK * BLK), :]
+            k = keys_of(n)
             vt = jnp.concatenate([vtc[n * (FAR_CHUNK // 2) + j] for j in range(FAR_CHUNK // 2)], axis=1)
-            scores = []
-            old = [(top[i, g], total[i, g]) for g in heads]
             for g in heads:
-                q = jnp.concatenate([qg[i, :, g * HEAD_DIM:(g + 1) * HEAD_DIM], mark], axis=1)
-                scores.append(lax.dot_general(k, q, (((1,), (1,)), ((), ())), preferred_element_type=jnp.float32))
-            done = []
-            for s, (peak_old, amount_old) in zip(scores, old):
-                s = s * SCALE
-                peak = jnp.maximum(peak_old, jnp.max(s, axis=0, keepdims=True))
-                shrink = jnp.exp2(peak_old - peak)
-                p = jnp.exp2(s - peak)
-                amount = amount_old * shrink + jnp.sum(p, axis=0, keepdims=True)
-                mix = jnp.dot(vt, p.astype(jnp.bfloat16), preferred_element_type=jnp.float32)
-                done.append((peak, amount, shrink, mix))
-            for g, (peak, amount, shrink, mix) in zip(heads, done):
-                top[i, g] = peak
-                total[i, g] = amount
-                acc[i, g] = acc[i, g] * shrink + mix
+                s = jnp.dot(k, qt[i, g], preferred_element_type=jnp.float32)
+                p = jnp.exp2(s * SCALE)
+                total[i, g] += jnp.sum(p, axis=0, keepdims=True)
+                acc[i, g] += jnp.dot(vt, p.astype(jnp.bfloat16), preferred_element_type=jnp.float32)
             return 0
 
         lax.fori_loop(0, chunks, chunk, 0)
@@ -344,20 +399,23 @@
 
     lax.fori_loop(0, tiles, swapped, 0)
     for d in range(1, SIDE):
-        pack_copy(d).wait_send()
+        for part in range(2):
+            pack_copy(part, d).wait_send()
         for copy in kv_copies(d):
             copy.wait_send()
         q_copy(d).wait_send()
         o_copy(peer(d), peer(d)).wait_send()
     for copy in next_copies():
         copy.wait_send()
-    own(sent)
-    for dp in (1, -1, 2):
-        first(dp, sent)
+    for part in range(2):
+        own(sent(part))
+        for dp in (1, -1, 2):
+            first(dp, sent(part))
 
     def ring_sent(step, _):
-        for dq in (1, -1):
-            second(step, dq, sent)
+        for part in range(2):
+            for dq in (1, -1):
+                second(step, dq, sent(part))
         return 0
 
     lax.fori_loop(0, SIDE, ring_sent, 0)
@@ -382,9 +440,10 @@
         in_specs=[vmem] * 3 + [smem] * 2 + [pl.BlockSpec(memory_space=pl.ANY)],
         out_specs=vmem,
         scratch_shapes=[
-            pltpu.VMEM((kv, 2 * CAP, BLK, HEAD_DIM), jnp.bfloat16),
-            pltpu.VMEM((n * 2 * CAP, BLK, HEAD_DIM), jnp.bfloat16),
+            [pltpu.VMEM((kv, CAP, BLK, HEAD_DIM), jnp.bfloat16) for _ in range(2)],
+            [pltpu.VMEM((n * CAP, BLK, HEAD_DIM), jnp.bfloat16) for _ in range(2)],
             pltpu.VMEM((SIDE, rows, width), jnp.bfloat16),
+            pltpu.VMEM((SIDE, per_group, 2 * HEAD_DIM, rows), jnp.bfloat16),
             pltpu.VMEM((SIDE + 1, rows, HEAD_DIM), jnp.bfloat16),
             pltpu.VMEM((SIDE + 1, rows, HEAD_DIM), jnp.bfloat16),
             pltpu.VMEM((listed * BLK, 2 * HEAD_DIM), jnp.bfloat16),
@@ -399,13 +458,13 @@
             pltpu.VMEM((tiles, rows // 2, tile), jnp.bfloat16),
             pltpu.VMEM((tiles, rows // 2, tile), jnp.bfloat16),
             dma,
-            dma((SIDE,)),
+            dma((2, SIDE)),
             dma((SIDE, 2)),
             dma((SIDE + 1, 2)),
             dma((SIDE,)),
             dma((SIDE,)),
-            dma((n,)),
-            dma((n, SIDE)),
+            dma((2, n)),
+            dma((2, n, SIDE)),
             dma((SIDE,)),
             dma((SIDE,)),
             dma((tiles,)),
@@ -414,7 +473,7 @@
         compiler_params=pltpu.CompilerParams(
             collective_id=0, has_side_effects=True, vmem_limit_bytes=60 * 2**20
         ),
-    )(queries, keys, values, vertical, slash, out_weight)
+    )(queries, keys, values, vertical, slash.T, out_weight)
 
 
 def solution(mesh):

time: 93.2 us -> 100 us (1.073)
  Pallas kernels: 89.2 us -> 97.6 us
  local copies, waits for them, and re-layouts: 3.62 us -> 2.29 us
    pallas_call x1, Pallas kernels: 89.2 us -> 97.6 us  [on_device(): pl.pallas_call(functools.partial(kernel, per_group, tile), out_shape=jax....]
    unnamed x2 -> x1, local copies, waits for them, and re-layouts: 3.62 us -> 2.29 us
where the time goes in v2:
time: 100 us; the launch traced here: 99.9 us
  Pallas kernels  97.6 us (98%)
  local copies, waits for them, and re-layouts  2.29 us (2%)
    pallas_call x1, Pallas kernels, on_device(): pl.pallas_call(functools.partial(kernel, per_group, tile), out_shape=jax....  97.6 us
    unnamed x1, local copies, waits for them, and re-layouts  2.29 us

profile of v2, /device:TPU:7, one launch (start us, length us, event | category | flops | bytes accessed | tf_op | source)
XLA Modules:
  0.0 99.9 jit_solution(7699634944080438467)
XLA Ops:
  0.0 97.6 %shard_map.64 = bf16[128,4096]{1,0:T(8,128)(2,1)} custom-call(bf16[256,2048]{1,0:T(8,128)(2,1)} %q_ref.1, bf16[256,512]{1,0:T(8,128)(2,1)} %k_ref.1, bf16[256,512]{1,0:T(8,128)(2,1)} %v_ref.1, s32[4,64]{1,0:T(4,128)} %vert_ref.1, s32[2,4]{1,0:T(2,128)} %bitcast.1, bf16[2048,4096]{1,0:T(8,128)(2,1)} %w_hbm.1), custom_call_target="tpu_custom_call" | custom-call | tf_op jit(solution)/shard_map/pallas_call | solution.py:437
  97.6 2.3 %copy.8 = bf16[128,4096]{1,0:T(8,128)(2,1)} copy(bf16[128,4096]{1,0:T(8,128)(2,1)} %shard_map.64) | data formatting | bytes 2097152

commit v3 on v2

--- a/solution.py
+++ b/solution.py
@@ -134,11 +134,11 @@
         return at(x + SIDE - dx, z + SIDE - dz, kind)
 
     def ring(part, slab, kind, phase, sign):
-        along_x = (kind < 2) == (phase == 0)
-        to = at(x + SIDE + sign, z, c) if along_x else at(x, z + SIDE + sign, c)
+        x_first = kind < 2
+        along_x = x_first if phase == 0 else jnp.logical_not(x_first)
+        to = jnp.where(along_x, at(x + SIDE + sign, z, c), at(x, z + SIDE + sign, c))
         there = held(part, slab)
-        way = (0 if along_x else 2) + (sign > 0)
-        return remote(there, there, ring_send.at[part, slab, way], slot_recv.at[part, slab], to)
+        return remote(there, there, ring_send.at[part], slot_recv.at[part, slab], to)
 
     def arrived(part, slab):
         there = held(part, slab)
@@ -146,11 +146,6 @@
 
     def sign_of(kind):
         return 1 if kind % 2 == 0 else -1
-
-    def own(act):
-        for kind in range(SIDE):
-            slab = slab_of(0, 0, kind)
-            act(slab, kind, [(0, 1), (0, -1), (1, 1), (1, -1)])
 
     def first(dp, act):
         for kind in range(SIDE):
@@ -170,27 +165,16 @@
         return act
 
     def pass_own(part):
-        def act(slab, kind, ways):
-            @pl.when(c != kind)
-            def _():
+        for d in (0, SIDE - 1, 1, 2):
+            slab = o * SIDE + peer(d)
+            if d:
                 arrived(part, slab)
-
-            for phase, sign in ways:
-                ring(part, slab, kind, phase, sign).start()
-
-        return act
-
-    def sent(part):
-        def act(slab, kind, ways):
-            for phase, sign in ways:
-                ring(part, slab, kind, phase, sign).wait_send()
-
-        return act
-
-    own(pass_own(0))
+            for phase, sign in ((0, 1), (0, -1), (1, 1), (1, -1)):
+                ring(part, slab, peer(d), phase, sign).start()
+
+    pass_own(0)
     for dp in (1, -1, 2):
         first(dp, pass_on(0))
-    own(pass_own(1))
 
     for d in range(1, SIDE):
         for i, got in enumerate((kg, vg)):
@@ -252,11 +236,11 @@
         lax.fori_loop(0, SIDE, one, 0)
 
     lax.fori_loop(0, SIDE, second_keys, 0)
+    pass_own(1)
     turn(c)
-    for dp in (1, -1, 2):
-        first(dp, pass_on(1))
     for copy in next_copies():
         copy.wait_recv()
+    near(c)
     last_ones(0)
 
     lane = lax.broadcasted_iota(jnp.int32, (BLK, HEAD_DIM), 1)
@@ -320,11 +304,30 @@
         def _():
             remote(qg.at[i], qg.at[i], q_send.at[1], q_recv.at[i], next_plane).wait_recv()
             turn(i)
-
-        for dq in (1, -1):
-            second(step, dq, pass_on(1))
-        near(i)
+            near(i)
+
         largest(i)
+
+        @pl.when(step == 0)
+        def _():
+            for dp in (1, -1):
+                first(dp, pass_on(1))
+
+        @pl.when(step == 1)
+        def _():
+            first(2, pass_on(1))
+            for dq in (1, -1):
+                second(0, dq, pass_on(1))
+
+        @pl.when(step == 2)
+        def _():
+            def rest(dp, _):
+                for dq in (1, -1):
+                    second(dp, dq, pass_on(1))
+                return 0
+
+            lax.fori_loop(1, SIDE, rest, 0)
+
         return 0
 
     lax.fori_loop(0, SIDE, first_pass, 0)
@@ -340,11 +343,17 @@
         def chunk(n, _):
             k = keys_of(n)
             vt = jnp.concatenate([vtc[n * (FAR_CHUNK // 2) + j] for j in range(FAR_CHUNK // 2)], axis=1)
-            for g in heads:
-                s = jnp.dot(k, qt[i, g], preferred_element_type=jnp.float32)
+            scores = [jnp.dot(k, qt[i, g], preferred_element_type=jnp.float32) for g in heads]
+            old = [(total[i, g], acc[i, g]) for g in heads]
+            new = []
+            for s, (amount, mix) in zip(scores, old):
                 p = jnp.exp2(s * SCALE)
-                total[i, g] += jnp.sum(p, axis=0, keepdims=True)
-                acc[i, g] += jnp.dot(vt, p.astype(jnp.bfloat16), preferred_element_type=jnp.float32)
+                amount = amount + jnp.sum(p, axis=0, keepdims=True)
+                mix = mix + jnp.dot(vt, p.astype(jnp.bfloat16), preferred_element_type=jnp.float32)
+                new.append((amount, mix))
+            for g, (amount, mix) in zip(heads, new):
+                total[i, g] = amount
+                acc[i, g] = mix
             return 0
 
         lax.fori_loop(0, chunks, chunk, 0)
@@ -408,17 +417,8 @@
     for copy in next_copies():
         copy.wait_send()
     for part in range(2):
-        own(sent(part))
-        for dp in (1, -1, 2):
-            first(dp, sent(part))
-
-    def ring_sent(step, _):
-        for part in range(2):
-            for dq in (1, -1):
-                second(step, dq, sent(part))
-        return 0
-
-    lax.fori_loop(0, SIDE, ring_sent, 0)
+        every = slots[part].at[pl.ds(0, (SIDE ** 3 - SIDE) * CAP)]
+        remote(every, every, ring_send.at[part], slot_recv.at[part, 0], next_plane).wait_send()
 
 
 def on_device(n, queries, keys, values, vertical, slash, out_weight):
@@ -429,7 +429,7 @@
     model = out_weight.shape[1]
     listed = vertical.shape[1]
 
-    tile = math.gcd(model, 512)
+    tile = math.gcd(model, 1024)
     tiles = model // tile
     vmem = pl.BlockSpec(memory_space=pltpu.VMEM)
     smem = pl.BlockSpec(memory_space=pltpu.SMEM)
@@ -464,7 +464,7 @@
             dma((SIDE,)),
             dma((SIDE,)),
             dma((2, n)),
-            dma((2, n, SIDE)),
+            dma((2,)),
             dma((SIDE,)),
             dma((SIDE,)),
             dma((tiles,)),

time: 100 us -> 79.2 us (0.79)
  Pallas kernels: 97.6 us -> 76.7 us
    pallas_call x1, Pallas kernels: 97.6 us -> 76.7 us  [on_device(): pl.pallas_call(functools.partial(kernel, per_group, tile), out_shape=jax....]
where the time goes in v3:
time: 79.2 us; the launch traced here: 79 us
  Pallas kernels  76.7 us (97%)
  local copies, waits for them, and re-layouts  2.29 us (3%)
    pallas_call x1, Pallas kernels, on_device(): pl.pallas_call(functools.partial(kernel, per_group, tile), out_shape=jax....  76.7 us
    unnamed x1, local copies, waits for them, and re-layouts  2.29 us

profile of v3, /device:TPU:7, one launch (start us, length us, event | category | flops | bytes accessed | tf_op | source)
XLA Modules:
  0.0 79.0 jit_solution(8023032582177613052)
XLA Ops:
  0.0 76.7 %shard_map.64 = bf16[128,4096]{1,0:T(8,128)(2,1)} custom-call(bf16[256,2048]{1,0:T(8,128)(2,1)} %q_ref.1, bf16[256,512]{1,0:T(8,128)(2,1)} %k_ref.1, bf16[256,512]{1,0:T(8,128)(2,1)} %v_ref.1, s32[4,64]{1,0:T(4,128)} %vert_ref.1, s32[2,4]{1,0:T(2,128)} %bitcast.1, bf16[2048,4096]{1,0:T(8,128)(2,1)} %w_hbm.1), custom_call_target="tpu_custom_call" | custom-call | tf_op jit(solution)/shard_map/pallas_call | solution.py:437
  76.7 2.3 %copy.8 = bf16[128,4096]{1,0:T(8,128)(2,1)} copy(bf16[128,4096]{1,0:T(8,128)(2,1)} %shard_map.64) | data formatting | bytes 2097152

commit v4 on v3

--- a/solution.py
+++ b/solution.py
@@ -15,16 +15,19 @@
 MESH = pl.DeviceIdType.MESH
 SCALE = HEAD_DIM ** (-0.5) * math.log2(math.e)
 SIDE = 4
-FAR_CHUNK = 16
+FAR_CHUNK = 32
+PAIRS = 2
+FAR_PARTS = 2
+TOP_CHUNK = 32
 AUX = 16
 
 
 def kernel(
     per_group, tile,
-    q_ref, k_ref, v_ref, vert_ref, slash_ref, w_hbm, out_ref,
-    packs, slots, qg, qt, kg, vg, kc, vtc, w_ref, acc, top, total, o_buf, attn, res, give, take,
+    q_ref, k_ref, v_ref, list_ref, vert_ref, slash_ref, w_hbm, out_ref,
+    packs, slots, qg, qt, kg, vg, aux_k, places, w_ref, acc, top, far_top, total, o_buf, attn, res, give, take, out_buf,
     w_sem, pack_send, kv_send, kv_recv, q_send, q_recv, slot_recv, ring_send,
-    o_send, o_recv, x_send, x_recv,
+    o_send, o_recv, x_send, x_recv, out_sem,
 ):
     rows = q_ref.shape[0]
     me = lax.axis_index("seq")
@@ -50,7 +53,7 @@
     greet(me, other)
     for d in range(1, SIDE):
         greet(o * SIDE + (c + d) % SIDE, core)
-    for step in (1, SIDE - 1):
+    for step in range(1, SIDE):
         greet(at(x + step, z, c), core)
         greet(at(x, z + step, c), core)
     greet(next_plane, core)
@@ -63,19 +66,18 @@
         return pl.ds(pl.multiple_of(h * size, size), size)
 
     first_block = me * slab_blocks
+    found = list_ref[...] - first_block
+    inside = (found >= 0) & (found < slab_blocks)
+    low = jnp.min(jnp.where(inside, found, slab_blocks), axis=1, keepdims=True)
+    high = jnp.max(jnp.where(inside, found, -1), axis=1, keepdims=True)
     for h in range(SIDE):
-        low, high = jnp.int32(slab_blocks), jnp.int32(-1)
-        for e in range(chosen_count):
-            block = vert_ref[h, e] - first_block
-            inside = (block >= 0) & (block < slab_blocks)
-            low = jnp.where(inside, jnp.minimum(low, block), low)
-            high = jnp.where(inside, jnp.maximum(high, block), high)
-        for slot, block in enumerate((low, high)):
+        for slot, extreme in enumerate((low, high)):
+            pick = jnp.broadcast_to(extreme[h:h + 1], (BLK, HEAD_DIM))
             for part, source in enumerate((k_ref, v_ref)):
                 got = source[:BLK, h * HEAD_DIM:(h + 1) * HEAD_DIM]
                 for i in range(1, slab_blocks):
                     rows_i = source[i * BLK:(i + 1) * BLK, h * HEAD_DIM:(h + 1) * HEAD_DIM]
-                    got = jnp.where(block == i, rows_i, got)
+                    got = jnp.where(pick == i, rows_i, got)
                 packs[part][h, slot] = got
     for part in range(2):
         for i in range(CAP):
@@ -84,7 +86,7 @@
     vg[c + 1] = v_ref[:, lanes(c)]
     qg[c] = q_ref[:, lanes(c, width)]
 
-    pl.semaphore_wait(barrier, 1 + (SIDE - 1) + 4 + 2)
+    pl.semaphore_wait(barrier, 1 + 3 * (SIDE - 1) + 2)
 
     def remote(src, dst, send_sem, recv_sem, seq):
         return pltpu.make_async_remote_copy(
@@ -120,18 +122,12 @@
         ]
 
     near_order = (1, SIDE - 1, 2)
-    for part in range(2):
-        for d in near_order:
-            pack_copy(part, d).start()
     for d in near_order:
-        for copy in kv_copies(d):
-            copy.start()
-    for d in near_order:
-        q_copy(d).start()
+        pack_copy(0, d).start()
 
     def slab_of(dp, dq, kind):
-        dx, dz = (dp, dq) if kind < 2 else (dq, dp)
-        return at(x + SIDE - dx, z + SIDE - dz, kind)
+        x_first = kind < 2
+        return jnp.where(x_first, at(x + SIDE - dp, z + SIDE - dq, kind), at(x + SIDE - dq, z + SIDE - dp, kind))
 
     def ring(part, slab, kind, phase, sign):
         x_first = kind < 2
@@ -147,10 +143,10 @@
     def sign_of(kind):
         return 1 if kind % 2 == 0 else -1
 
-    def first(dp, act):
-        for kind in range(SIDE):
-            ways = [(0, dp)] if dp == sign_of(kind) else []
-            act(slab_of(dp, 0, kind), kind, ways + [(1, 1), (1, -1)])
+    def first(act):
+        for d in (0, SIDE - 1, 1, 2):
+            for dp in (1, -1, 2):
+                act(slab_of(dp, 0, peer(d)), peer(d), [(1, 1), (1, -1)])
 
     def second(dp, dq, act):
         for kind in range(SIDE):
@@ -169,19 +165,34 @@
             slab = o * SIDE + peer(d)
             if d:
                 arrived(part, slab)
-            for phase, sign in ((0, 1), (0, -1), (1, 1), (1, -1)):
+            for phase, sign in ((0, 1), (0, -1), (0, 2), (1, 1), (1, -1)):
                 ring(part, slab, peer(d), phase, sign).start()
 
     pass_own(0)
-    for dp in (1, -1, 2):
-        first(dp, pass_on(0))
-
-    for d in range(1, SIDE):
-        for i, got in enumerate((kg, vg)):
-            there = got.at[peer(d) + 1]
-            remote(there, there, kv_send.at[d, i], kv_recv.at[peer(d) + 1, i], next_plane).wait_recv()
-    for copy in next_copies():
-        copy.start()
+    for d in near_order:
+        for copy in kv_copies(d):
+            copy.start()
+    for d in near_order:
+        pack_copy(1, d).start()
+    for d in (SIDE - 1, 1, 2):
+        q_copy(d).start()
+    lane = lax.broadcasted_iota(jnp.int32, (BLK, HEAD_DIM), 1)
+    limit = (o * SIDE + lane - 1) * slab_blocks
+    unit = jnp.where((lane >= SIDE) & (lane < SIDE + 3), 1.0, 0.0)
+
+    def look_up(n, _):
+        for j in range(8):
+            e = n * 8 + j
+            block = vert_ref[c, e]
+            slab = block // slab_blocks
+            before = jnp.where(e > 0, vert_ref[c, jnp.maximum(e - 1, 0)] // slab_blocks, -1)
+            places[e] = slab * CAP + jnp.where(before == slab, 1, 0)
+            mask = jnp.where((lane < SIDE) & (block >= limit), NEGATIVE, unit)
+            aux_k[pl.ds(pl.multiple_of(e * BLK, BLK), BLK), :] = mask.astype(jnp.bfloat16)
+        return 0
+
+    lax.fori_loop(0, chosen_count // 8, look_up, 0)
+    first(pass_on(0))
 
     heads = range(per_group)
 
@@ -237,53 +248,51 @@
 
     lax.fori_loop(0, SIDE, second_keys, 0)
     pass_own(1)
+    for d in range(1, SIDE):
+        for i, got in enumerate((kg, vg)):
+            there = got.at[peer(d) + 1]
+            remote(there, there, kv_send.at[d, i], kv_recv.at[peer(d) + 1, i], next_plane).wait_recv()
+    for copy in next_copies():
+        copy.start()
+
+    def queries_in(i):
+        remote(qg.at[i], qg.at[i], q_send.at[1], q_recv.at[i], next_plane).wait_recv()
+
     turn(c)
-    for copy in next_copies():
-        copy.wait_recv()
-    near(c)
+
+    @pl.when(c > 0)
+    def _():
+        near(c)
+
     last_ones(0)
 
-    lane = lax.broadcasted_iota(jnp.int32, (BLK, HEAD_DIM), 1)
-    limit = (o * SIDE + lane - 1) * slab_blocks
-    unit = jnp.where((lane >= SIDE) & (lane < SIDE + 3), 1.0, 0.0)
-    chunks = jnp.minimum(chosen_count // FAR_CHUNK, (o + 2) // 2)
-
-    def place(e):
-        slab = vert_ref[c, e] // slab_blocks
-        before = jnp.where(e > 0, vert_ref[c, jnp.maximum(e - 1, 0)] // slab_blocks, -1)
-        return slab * CAP + jnp.where(before == slab, 1, 0)
-
-    def collect_keys(n, _):
-        for j in range(8):
-            e = n * 8 + j
-            at_row = pl.ds(pl.multiple_of(e * BLK, BLK), BLK)
-            kc[at_row, :HEAD_DIM] = slots[0][place(e)]
-            mask = jnp.where((lane < SIDE) & (vert_ref[c, e] >= limit), NEGATIVE, unit)
-            kc[at_row, HEAD_DIM:] = mask.astype(jnp.bfloat16)
-        return 0
-
-    def collect_values(n, _):
-        for j in range(4):
-            pair = n * 4 + j
-            both = jnp.concatenate([slots[1][place(pair * 2)], slots[1][place(pair * 2 + 1)]], axis=0)
-            vtc[pair] = both.T
-        return 0
-
-    def keys_of(n):
-        return kc[pl.ds(pl.multiple_of(n * FAR_CHUNK * BLK, FAR_CHUNK * BLK), FAR_CHUNK * BLK), :]
+    def blocks(part, n, size):
+        return jnp.concatenate([slots[part][places[n * size + j]] for j in range(size)], axis=0)
+
+    def keys_of(n, size):
+        masks = aux_k[pl.ds(pl.multiple_of(n * size * BLK, size * BLK), size * BLK), :]
+        return jnp.concatenate([blocks(0, n, size), masks], axis=1)
+
+    def steps(size):
+        return jnp.minimum(chosen_count, (o * SIDE + 2) * CAP + size - 1) // size
 
     def largest(i):
         def chunk(n, peaks):
-            k = keys_of(n)
+            k = keys_of(n, TOP_CHUNK)
             return tuple(
                 jnp.maximum(peak, jnp.max(jnp.dot(k, qt[i, g], preferred_element_type=jnp.float32),
                                           axis=0, keepdims=True))
                 for g, peak in zip(heads, peaks))
 
-        near_peaks = tuple(top[i, g] for g in heads)
-        peaks = lax.fori_loop(0, chunks, chunk, near_peaks)
+        peaks = lax.fori_loop(0, steps(TOP_CHUNK), chunk, (jnp.full((1, rows), NEGATIVE),) * per_group)
+        for g, peak in zip(heads, peaks):
+            far_top[i, g] = peak
+
+    def join(i):
         row = lax.broadcasted_iota(jnp.int32, (AUX, rows), 0)
-        for g, peak, old in zip(heads, peaks, near_peaks):
+        for g in heads:
+            old = top[i, g]
+            peak = jnp.maximum(old, far_top[i, g])
             shrink = jnp.exp2((old - peak) * SCALE)
             total[i, g] = total[i, g] * shrink
             acc[i, g] = acc[i, g] * shrink
@@ -295,29 +304,19 @@
                 rest = rest - part
             qt[i, g, HEAD_DIM:HEAD_DIM + AUX] = aux.astype(jnp.bfloat16)
 
-    lax.fori_loop(0, chunks * (FAR_CHUNK // 8), collect_keys, 0)
-
     def first_pass(step, _):
-        i = (c + step) % SIDE
+        i = (c + step + jnp.where(step == 2, 1, jnp.where(step == 3, -1, 0))) % SIDE
 
         @pl.when(step > 0)
         def _():
-            remote(qg.at[i], qg.at[i], q_send.at[1], q_recv.at[i], next_plane).wait_recv()
+            queries_in(i)
             turn(i)
-            near(i)
 
         largest(i)
 
         @pl.when(step == 0)
         def _():
-            for dp in (1, -1):
-                first(dp, pass_on(1))
-
-        @pl.when(step == 1)
-        def _():
-            first(2, pass_on(1))
-            for dq in (1, -1):
-                second(0, dq, pass_on(1))
+            first(pass_on(1))
 
         @pl.when(step == 2)
         def _():
@@ -326,52 +325,72 @@
                     second(dp, dq, pass_on(1))
                 return 0
 
-            lax.fori_loop(1, SIDE, rest, 0)
+            lax.fori_loop(0, SIDE, rest, 0)
 
         return 0
 
     lax.fori_loop(0, SIDE, first_pass, 0)
+    for copy in next_copies():
+        copy.wait_recv()
+
+    def other_near(i, _):
+        @pl.when((i != c) | (c == 0))
+        def _():
+            near(i)
+
+        return 0
+
+    lax.fori_loop(0, SIDE, other_near, 0)
     last_ones(1)
-    lax.fori_loop(0, chunks * (FAR_CHUNK // 8), collect_values, 0)
-
-    def o_copy(i, to):
-        return remote(o_buf.at[i], attn.at[c], o_send.at[i], o_recv.at[c], o * SIDE + to)
+
+    def o_copies(i, pair):
+        columns = pl.ds(pair * width // PAIRS, width // PAIRS)
+        return remote(o_buf.at[i, :, columns], attn.at[c, :, columns], o_send.at[i, pair], o_recv.at[c, pair], o * SIDE + i)
 
     def far_slab(step, _):
         i = (c + SIDE - 1 - step) % SIDE
-
-        def chunk(n, _):
-            k = keys_of(n)
-            vt = jnp.concatenate([vtc[n * (FAR_CHUNK // 2) + j] for j in range(FAR_CHUNK // 2)], axis=1)
-            scores = [jnp.dot(k, qt[i, g], preferred_element_type=jnp.float32) for g in heads]
-            old = [(total[i, g], acc[i, g]) for g in heads]
-            new = []
-            for s, (amount, mix) in zip(scores, old):
-                p = jnp.exp2(s * SCALE)
-                amount = amount + jnp.sum(p, axis=0, keepdims=True)
-                mix = mix + jnp.dot(vt, p.astype(jnp.bfloat16), preferred_element_type=jnp.float32)
-                new.append((amount, mix))
-            for g, (amount, mix) in zip(heads, new):
-                total[i, g] = amount
-                acc[i, g] = mix
-            return 0
-
-        lax.fori_loop(0, chunks, chunk, 0)
-        for g in heads:
-            a = acc[i, g] * (1.0 / total[i, g])
-            o_buf[i, :, g * HEAD_DIM:(g + 1) * HEAD_DIM] = a.T.astype(jnp.bfloat16)
-
-        @pl.when(step < SIDE - 1)
-        def _():
-            o_copy(i, i).start()
+        join(i)
+        for pair in range(PAIRS):
+            some = heads[pair * per_group // PAIRS:(pair + 1) * per_group // PAIRS]
+
+            def part_of_list(n):
+                k = keys_of(n, FAR_CHUNK)
+                v = blocks(1, n, FAR_CHUNK)
+                scores = [jnp.dot(k, qt[i, g], preferred_element_type=jnp.float32) for g in some]
+                old = [(total[i, g], acc[i, g]) for g in some]
+                new = []
+                for s, (amount, mix) in zip(scores, old):
+                    p = jnp.exp2(s * SCALE)
+                    amount = amount + jnp.sum(p, axis=0, keepdims=True)
+                    mix = mix + lax.dot_general(v, p.astype(jnp.bfloat16), (((0,), (0,)), ((), ())),
+                                                preferred_element_type=jnp.float32)
+                    new.append((amount, mix))
+                for g, (amount, mix) in zip(some, new):
+                    total[i, g] = amount
+                    acc[i, g] = mix
+
+            def chunk(n, _):
+                for j in range(FAR_PARTS):
+                    part_of_list(n * FAR_PARTS + j)
+                return 0
+
+            lax.fori_loop(0, steps(FAR_CHUNK * FAR_PARTS), chunk, 0)
+            for g in some:
+                a = acc[i, g] * (1.0 / total[i, g])
+                o_buf[i, :, g * HEAD_DIM:(g + 1) * HEAD_DIM] = a.T.astype(jnp.bfloat16)
+
+            @pl.when(step < SIDE - 1)
+            def _():
+                o_copies(i, pair).start()
 
         return 0
 
     lax.fori_loop(0, SIDE, far_slab, 0)
     attn[c] = o_buf[c]
     for d in range(1, SIDE):
-        there = attn.at[peer(d)]
-        remote(there, there, o_send.at[peer(d)], o_recv.at[peer(d)], next_plane).wait_recv()
+        for pair in range(PAIRS):
+            there = attn.at[peer(d), :, pl.ds(pair * width // PAIRS, width // PAIRS)]
+            remote(there, there, o_send.at[peer(d), pair], o_recv.at[peer(d), pair], next_plane).wait_recv()
 
     weight_copy.wait()
     tiles = give.shape[0]
@@ -394,10 +413,15 @@
 
     lax.fori_loop(0, tiles, project, 0)
 
+    def put(t):
+        columns = pl.ds(pl.multiple_of(t * tile, tile), tile)
+        return pltpu.make_async_copy(out_buf.at[:, columns], out_ref.at[:, columns], out_sem.at[t])
+
     def add_up(t, _):
         columns = pl.ds(pl.multiple_of(t * tile, tile), tile)
         swap(t).wait_recv()
-        out_ref[:, columns] = (res[t, mine, :] + take[t].astype(jnp.float32)).astype(out_ref.dtype)
+        out_buf[:, columns] = (res[t, mine, :] + take[t].astype(jnp.float32)).astype(out_ref.dtype)
+        put(t).start()
         return 0
 
     lax.fori_loop(0, tiles, add_up, 0)
@@ -413,12 +437,19 @@
         for copy in kv_copies(d):
             copy.wait_send()
         q_copy(d).wait_send()
-        o_copy(peer(d), peer(d)).wait_send()
+        for pair in range(PAIRS):
+            o_copies(peer(d), pair).wait_send()
     for copy in next_copies():
         copy.wait_send()
     for part in range(2):
         every = slots[part].at[pl.ds(0, (SIDE ** 3 - SIDE) * CAP)]
         remote(every, every, ring_send.at[part], slot_recv.at[part, 0], next_plane).wait_send()
+
+    def stored(t, _):
+        put(t).wait()
+        return 0
+
+    lax.fori_loop(0, tiles, stored, 0)
 
 
 def on_device(n, queries, keys, values, vertical, slash, out_weight):
@@ -437,8 +468,8 @@
     return pl.pallas_call(
         functools.partial(kernel, per_group, tile),
         out_shape=jax.ShapeDtypeStruct((rows // 2, model), jnp.bfloat16),
-        in_specs=[vmem] * 3 + [smem] * 2 + [pl.BlockSpec(memory_space=pl.ANY)],
-        out_specs=vmem,
+        in_specs=[vmem] * 4 + [smem] * 2 + [pl.BlockSpec(memory_space=pl.ANY)],
+        out_specs=pl.BlockSpec(memory_space=pl.ANY),
         scratch_shapes=[
             [pltpu.VMEM((kv, CAP, BLK, HEAD_DIM), jnp.bfloat16) for _ in range(2)],
             [pltpu.VMEM((n * CAP, BLK, HEAD_DIM), jnp.bfloat16) for _ in range(2)],
@@ -446,10 +477,11 @@
             pltpu.VMEM((SIDE, per_group, 2 * HEAD_DIM, rows), jnp.bfloat16),
             pltpu.VMEM((SIDE + 1, rows, HEAD_DIM), jnp.bfloat16),
             pltpu.VMEM((SIDE + 1, rows, HEAD_DIM), jnp.bfloat16),
-            pltpu.VMEM((listed * BLK, 2 * HEAD_DIM), jnp.bfloat16),
-            pltpu.VMEM((listed // 2, HEAD_DIM, 2 * BLK), jnp.bfloat16),
+            pltpu.VMEM((listed * BLK, HEAD_DIM), jnp.bfloat16),
+            pltpu.SMEM((listed,), jnp.int32),
             pltpu.VMEM(out_weight.shape, jnp.bfloat16),
             pltpu.VMEM((SIDE, per_group, HEAD_DIM, rows), jnp.float32),
+            pltpu.VMEM((SIDE, per_group, 1, rows), jnp.float32),
             pltpu.VMEM((SIDE, per_group, 1, rows), jnp.float32),
             pltpu.VMEM((SIDE, per_group, 1, rows), jnp.float32),
             pltpu.VMEM((SIDE, rows, width), jnp.bfloat16),
@@ -457,6 +489,7 @@
             pltpu.VMEM((tiles, rows, tile), jnp.float32),
             pltpu.VMEM((tiles, rows // 2, tile), jnp.bfloat16),
             pltpu.VMEM((tiles, rows // 2, tile), jnp.bfloat16),
+            pltpu.VMEM((rows // 2, model), jnp.bfloat16),
             dma,
             dma((2, SIDE)),
             dma((SIDE, 2)),
@@ -465,15 +498,16 @@
             dma((SIDE,)),
             dma((2, n)),
             dma((2,)),
-            dma((SIDE,)),
-            dma((SIDE,)),
+            dma((SIDE, PAIRS)),
+            dma((SIDE, PAIRS)),
+            dma((tiles,)),
             dma((tiles,)),
             dma((tiles,)),
         ],
         compiler_params=pltpu.CompilerParams(
             collective_id=0, has_side_effects=True, vmem_limit_bytes=60 * 2**20
         ),
-    )(queries, keys, values, vertical, slash.T, out_weight)
+    )(queries, keys, values, vertical, vertical, slash.T, out_weight)
 
 
 def solution(mesh):

time: 79.2 us -> 71.2 us (0.90); the launches traced: 79 us -> 69.8 us
  Pallas kernels: 76.7 us -> 67.5 us
    pallas_call x1, Pallas kernels: 76.7 us -> 67.5 us  [on_device(): pl.pallas_call(functools.partial(kernel, per_group, tile), out_shape=jax....]
where the time goes in v4:
time: 71.2 us; the launch traced here: 69.8 us
  Pallas kernels  67.5 us (95%)
  local copies, waits for them, and re-layouts  2.29 us (3%)
    pallas_call x1, Pallas kernels, on_device(): pl.pallas_call(functools.partial(kernel, per_group, tile), out_shape=jax....  67.5 us
    unnamed x1, local copies, waits for them, and re-layouts  2.29 us

profile of v4, /device:TPU:7, one launch (start us, length us, event | category | flops | bytes accessed | tf_op | source)
XLA Modules:
  0.0 69.8 jit_solution(3327600992804707553)
XLA Ops:
  0.0 67.5 %shard_map.64 = bf16[128,4096]{1,0:T(8,128)(2,1)} custom-call(bf16[256,2048]{1,0:T(8,128)(2,1)} %q_ref.1, bf16[256,512]{1,0:T(8,128)(2,1)} %k_ref.1, bf16[256,512]{1,0:T(8,128)(2,1)} %v_ref.1, s32[4,64]{1,0:T(4,128)} %vert_ref.1, s32[4,64]{1,0:T(4,128)} %vert_ref.1, s32[2,4]{1,0:T(2,128)} %bitcast.1, bf16[2048,4096]{1,0:T(8,128)(2,1)} %w_hbm.1), custom_call_target="tpu_custom_call" | custom-call | tf_op jit(solution)/shard_map/pallas_call | solution.py:468
  67.5 2.3 %copy.8 = bf16[128,4096]{1,0:T(8,128)(2,1)} copy(bf16[128,4096]{1,0:T(8,128)(2,1)} %shard_map.64) | data formatting | bytes 2097152

commit v5 on v4

--- a/solution.py
+++ b/solution.py
@@ -18,15 +18,17 @@
 FAR_CHUNK = 32
 PAIRS = 2
 FAR_PARTS = 2
+ENDS = 2 * SIDE * SIDE
 TOP_CHUNK = 32
 AUX = 16
 
 
 def kernel(
     per_group, tile,
-    q_ref, k_ref, v_ref, list_ref, vert_ref, slash_ref, w_hbm, out_ref,
-    packs, slots, qg, qt, kg, vg, aux_k, places, w_ref, acc, top, far_top, total, o_buf, attn, res, give, take, out_buf,
-    w_sem, pack_send, kv_send, kv_recv, q_send, q_recv, slot_recv, ring_send,
+    q_hbm, k_hbm, v_hbm, vert_hbm, slash_hbm, w_hbm, out_ref,
+    q_ref, k_ref, v_ref, list_ref, vert_ref, slash_ref,
+    packs, slots, qg, qt, kg, vg, aux_k, places, w_ref, acc, top, far_top, total, o_buf, attn, give, take, out_buf,
+    in_sem, w_sem, pack_send, kv_send, kv_recv, q_send, q_recv, slot_recv, ring_send,
     o_send, o_recv, x_send, x_recv, out_sem,
 ):
     rows = q_ref.shape[0]
@@ -45,6 +47,15 @@
     def at(xx, zz, cc):
         return (xx % SIDE * SIDE + zz % SIDE) * SIDE + cc
 
+    given = [
+        pltpu.make_async_copy(source, here, in_sem.at[i])
+        for i, (source, here) in enumerate((
+            (vert_hbm, list_ref), (k_hbm, k_ref), (v_hbm, v_ref), (q_hbm, q_ref), (vert_hbm, vert_ref),
+            (slash_hbm, slash_ref)))
+    ]
+    for copy in given:
+        copy.start()
+
     barrier = pltpu.get_barrier_semaphore()
 
     def greet(seq, head):
@@ -66,6 +77,8 @@
         return pl.ds(pl.multiple_of(h * size, size), size)
 
     first_block = me * slab_blocks
+    for copy in given:
+        copy.wait()
     found = list_ref[...] - first_block
     inside = (found >= 0) & (found < slab_blocks)
     low = jnp.min(jnp.where(inside, found, slab_blocks), axis=1, keepdims=True)
@@ -101,7 +114,7 @@
         return (c + d) % SIDE
 
     def pack_copy(part, d):
-        return remote(packs[part].at[peer(d)], held(part, me), pack_send.at[part, d], slot_recv.at[part, me],
+        return remote(packs[part].at[peer(d)], held(part, me), pack_send.at[part, d], slot_recv.at[part, c],
                       o * SIDE + peer(d))
 
     def kv_copies(d):
@@ -129,53 +142,54 @@
         x_first = kind < 2
         return jnp.where(x_first, at(x + SIDE - dp, z + SIDE - dq, kind), at(x + SIDE - dq, z + SIDE - dp, kind))
 
-    def ring(part, slab, kind, phase, sign):
+    def ring(part, slab, kind, phase, sign, mark):
         x_first = kind < 2
         along_x = x_first if phase == 0 else jnp.logical_not(x_first)
         to = jnp.where(along_x, at(x + SIDE + sign, z, c), at(x, z + SIDE + sign, c))
         there = held(part, slab)
-        return remote(there, there, ring_send.at[part], slot_recv.at[part, slab], to)
-
-    def arrived(part, slab):
+        return remote(there, there, ring_send.at[part], slot_recv.at[part, mark], to)
+
+    def in_group(kind):
+        return kind
+
+    def in_first(dp, kind):
+        return SIDE + (dp % SIDE - 1) * SIDE + kind
+
+    def in_second(dp, sign, kind):
+        return jnp.where(kind % 2 == (1 - sign) // 2, SIDE * (SIDE + dp % SIDE) + kind, ENDS)
+
+    def arrived(part, slab, mark):
         there = held(part, slab)
-        remote(there, there, pack_send.at[part, 1], slot_recv.at[part, slab], next_plane).wait_recv()
-
-    def sign_of(kind):
-        return 1 if kind % 2 == 0 else -1
-
-    def first(act):
-        for d in (0, SIDE - 1, 1, 2):
+        remote(there, there, pack_send.at[part, 1], slot_recv.at[part, mark], next_plane).wait_recv()
+
+    def first(part, ds=(0, SIDE - 1, 1, 2)):
+        for d in ds:
+            kind = peer(d)
             for dp in (1, -1, 2):
-                act(slab_of(dp, 0, peer(d)), peer(d), [(1, 1), (1, -1)])
-
-    def second(dp, dq, act):
+                slab = slab_of(dp, 0, kind)
+                arrived(part, slab, in_first(dp, kind))
+                for sign in (1, -1):
+                    ring(part, slab, kind, 1, sign, in_second(dp, sign, kind)).start()
+
+    def second(part, dp):
         for kind in range(SIDE):
-            act(slab_of(dp, dq, kind), kind, [(1, dq)] if dq == sign_of(kind) else [])
-
-    def pass_on(part):
-        def act(slab, kind, ways):
-            arrived(part, slab)
-            for phase, sign in ways:
-                ring(part, slab, kind, phase, sign).start()
-
-        return act
-
-    def pass_own(part):
-        for d in (0, SIDE - 1, 1, 2):
+            sign = 1 if kind % 2 == 0 else -1
+            slab = slab_of(dp, sign, kind)
+            arrived(part, slab, in_second(dp, sign, kind))
+            ring(part, slab, kind, 1, sign, ENDS).start()
+
+    def pass_own(part, ds):
+        for d in ds:
             slab = o * SIDE + peer(d)
+            kind = peer(d)
             if d:
-                arrived(part, slab)
-            for phase, sign in ((0, 1), (0, -1), (0, 2), (1, 1), (1, -1)):
-                ring(part, slab, peer(d), phase, sign).start()
-
-    pass_own(0)
-    for d in near_order:
-        for copy in kv_copies(d):
-            copy.start()
-    for d in near_order:
-        pack_copy(1, d).start()
-    for d in (SIDE - 1, 1, 2):
-        q_copy(d).start()
+                arrived(part, slab, in_group(kind))
+            for step in (1, -1, 2):
+                ring(part, slab, kind, 0, step, in_first(step, kind)).start()
+            for sign in (1, -1):
+                ring(part, slab, kind, 1, sign, in_second(0, sign, kind)).start()
+
+    pass_own(0, (0,))
     lane = lax.broadcasted_iota(jnp.int32, (BLK, HEAD_DIM), 1)
     limit = (o * SIDE + lane - 1) * slab_blocks
     unit = jnp.where((lane >= SIDE) & (lane < SIDE + 3), 1.0, 0.0)
@@ -192,7 +206,15 @@
         return 0
 
     lax.fori_loop(0, chosen_count // 8, look_up, 0)
-    first(pass_on(0))
+    pass_own(0, (SIDE - 1, 1, 2))
+    for d in near_order:
+        for copy in kv_copies(d):
+            copy.start()
+    for d in near_order:
+        pack_copy(1, d).start()
+    for d in (SIDE - 1, 1, 2):
+        q_copy(d).start()
+    first(0)
 
     heads = range(per_group)
 
@@ -234,20 +256,16 @@
             total[i, g] = jnp.sum(p, axis=0, keepdims=True)
             acc[i, g] = jnp.dot(vt, p.astype(jnp.bfloat16), preferred_element_type=jnp.float32)
 
-    def second_keys(step, _):
-        for dq in (1, -1):
-            second(step, dq, pass_on(0))
+    def second_keys(dp, _):
+        second(0, dp)
         return 0
 
     def last_ones(part):
-        def one(step, _):
-            second(step, 2, lambda slab, kind, ways: arrived(part, slab))
-            return 0
-
-        lax.fori_loop(0, SIDE, one, 0)
+        every = slots[part].at[pl.ds(0, 2 * SIDE * SIDE * CAP)]
+        remote(every, every, pack_send.at[part, 1], slot_recv.at[part, ENDS], next_plane).wait_recv()
 
     lax.fori_loop(0, SIDE, second_keys, 0)
-    pass_own(1)
+    pass_own(1, (0, SIDE - 1, 1, 2))
     for d in range(1, SIDE):
         for i, got in enumerate((kg, vg)):
             there = got.at[peer(d) + 1]
@@ -316,17 +334,18 @@
 
         @pl.when(step == 0)
         def _():
-            first(pass_on(1))
-
-        @pl.when(step == 2)
+            first(1, (0, SIDE - 1))
+
+        @pl.when(step == 1)
         def _():
-            def rest(dp, _):
-                for dq in (1, -1):
-                    second(dp, dq, pass_on(1))
-                return 0
-
-            lax.fori_loop(0, SIDE, rest, 0)
-
+            first(1, (1, 2))
+
+        def values_second(j, _):
+            second(1, (2 + j) % SIDE)
+            return 0
+
+        lax.fori_loop(jnp.where(step == 2, 1, jnp.where(step == 3, 0, SIDE)),
+                      jnp.where(step == 3, 1, SIDE), values_second, 0)
         return 0
 
     lax.fori_loop(0, SIDE, first_pass, 0)
@@ -334,7 +353,7 @@
         copy.wait_recv()
 
     def other_near(i, _):
-        @pl.when((i != c) | (c == 0))
+        @pl.when(i != c)
         def _():
             near(i)
 
@@ -349,6 +368,11 @@
 
     def far_slab(step, _):
         i = (c + SIDE - 1 - step) % SIDE
+
+        @pl.when((step == SIDE - 1) & (c == 0))
+        def _():
+            near(i)
+
         join(i)
         for pair in range(PAIRS):
             some = heads[pair * per_group // PAIRS:(pair + 1) * per_group // PAIRS]
@@ -403,15 +427,17 @@
             device_id=(me, other), device_id_type=MESH,
         )
 
-    def project(t, _):
+    def project(t, place):
         columns = pl.ds(pl.multiple_of(t * tile, tile), tile)
-        a = jnp.concatenate([attn[j] for j in range(SIDE)], axis=1)
-        res[t] = jnp.dot(a, w_ref[:, columns], preferred_element_type=jnp.float32)
-        give[t] = res[t, theirs, :].astype(jnp.bfloat16)
+        a = jnp.concatenate([attn[j, place, :] for j in range(SIDE)], axis=1)
+        return jnp.dot(a, w_ref[:, columns], preferred_element_type=jnp.float32)
+
+    def share(t, _):
+        give[t] = project(t, theirs).astype(jnp.bfloat16)
         swap(t).start()
         return 0
 
-    lax.fori_loop(0, tiles, project, 0)
+    lax.fori_loop(0, tiles, share, 0)
 
     def put(t):
         columns = pl.ds(pl.multiple_of(t * tile, tile), tile)
@@ -420,7 +446,7 @@
     def add_up(t, _):
         columns = pl.ds(pl.multiple_of(t * tile, tile), tile)
         swap(t).wait_recv()
-        out_buf[:, columns] = (res[t, mine, :] + take[t].astype(jnp.float32)).astype(out_ref.dtype)
+        out_buf[:, columns] = (project(t, mine) + take[t].astype(jnp.float32)).astype(out_ref.dtype)
         put(t).start()
         return 0
 
@@ -462,15 +488,19 @@
 
     tile = math.gcd(model, 1024)
     tiles = model // tile
-    vmem = pl.BlockSpec(memory_space=pltpu.VMEM)
-    smem = pl.BlockSpec(memory_space=pltpu.SMEM)
     dma = pltpu.SemaphoreType.DMA
     return pl.pallas_call(
         functools.partial(kernel, per_group, tile),
         out_shape=jax.ShapeDtypeStruct((rows // 2, model), jnp.bfloat16),
-        in_specs=[vmem] * 4 + [smem] * 2 + [pl.BlockSpec(memory_space=pl.ANY)],
+        in_specs=[pl.BlockSpec(memory_space=pl.ANY)] * 6,
         out_specs=pl.BlockSpec(memory_space=pl.ANY),
         scratch_shapes=[
+            pltpu.VMEM(queries.shape, jnp.bfloat16),
+            pltpu.VMEM(keys.shape, jnp.bfloat16),
+            pltpu.VMEM(values.shape, jnp.bfloat16),
+            pltpu.VMEM(vertical.shape, jnp.int32),
+            pltpu.SMEM(vertical.shape, jnp.int32),
+            pltpu.SMEM(slash.T.shape, jnp.int32),
             [pltpu.VMEM((kv, CAP, BLK, HEAD_DIM), jnp.bfloat16) for _ in range(2)],
             [pltpu.VMEM((n * CAP, BLK, HEAD_DIM), jnp.bfloat16) for _ in range(2)],
             pltpu.VMEM((SIDE, rows, width), jnp.bfloat16),
@@ -486,17 +516,17 @@
             pltpu.VMEM((SIDE, per_group, 1, rows), jnp.float32),
             pltpu.VMEM((SIDE, rows, width), jnp.bfloat16),
             pltpu.VMEM((SIDE, rows, width), jnp.bfloat16),
-            pltpu.VMEM((tiles, rows, tile), jnp.float32),
             pltpu.VMEM((tiles, rows // 2, tile), jnp.bfloat16),
             pltpu.VMEM((tiles, rows // 2, tile), jnp.bfloat16),
             pltpu.VMEM((rows // 2, model), jnp.bfloat16),
+            dma((6,)),
             dma,
             dma((2, SIDE)),
             dma((SIDE, 2)),
             dma((SIDE + 1, 2)),
             dma((SIDE,)),
             dma((SIDE,)),
-            dma((2, n)),
+            dma((2, ENDS + 1)),
             dma((2,)),
             dma((SIDE, PAIRS)),
             dma((SIDE, PAIRS)),
@@ -507,7 +537,7 @@
         compiler_params=pltpu.CompilerParams(
             collective_id=0, has_side_effects=True, vmem_limit_bytes=60 * 2**20
         ),
-    )(queries, keys, values, vertical, vertical, slash.T, out_weight)
+    )(queries, keys, values, vertical, slash.T, out_weight)
 
 
 def solution(mesh):

time: 71.2 us -> 68.8 us (0.966); the launches traced: 69.8 us -> 68.2 us
  Pallas kernels: 67.5 us -> 65.9 us
    pallas_call x1, Pallas kernels: 67.5 us -> 65.9 us  [on_device(): pl.pallas_call(functools.partial(kernel, per_group, tile), out_shape=jax....]
where the time goes in v5:
time: 68.8 us; the launch traced here: 68.2 us
  Pallas kernels  65.9 us (96%)
  local copies, waits for them, and re-layouts  2.29 us (3%)
    pallas_call x1, Pallas kernels, on_device(): pl.pallas_call(functools.partial(kernel, per_group, tile), out_shape=jax....  65.9 us
    unnamed x1, local copies, waits for them, and re-layouts  2.29 us

profile of v5, /device:TPU:7, one launch (start us, length us, event | category | flops | bytes accessed | tf_op | source)
XLA Modules:
  0.0 68.2 jit_solution(9806607329513238462)
XLA Ops:
  0.0 65.9 %shard_map.64 = bf16[128,4096]{1,0:T(8,128)(2,1)} custom-call(bf16[256,2048]{1,0:T(8,128)(2,1)} %q_hbm.1, bf16[256,512]{1,0:T(8,128)(2,1)} %k_hbm.1, bf16[256,512]{1,0:T(8,128)(2,1)} %v_hbm.1, s32[4,64]{1,0:T(4,128)} %vert_hbm.1, s32[2,4]{1,0:T(2,128)} %bitcast.1, bf16[2048,4096]{1,0:T(8,128)(2,1)} %w_hbm.1), custom_call_target="tpu_custom_call" | custom-call | tf_op jit(solution)/shard_map/pallas_call | solution.py:492
  65.9 2.3 %copy.8 = bf16[128,4096]{1,0:T(8,128)(2,1)} copy(bf16[128,4096]{1,0:T(8,128)(2,1)} %shard_map.64) | data formatting | bytes 2097152

commit v6 on v5

--- a/solution.py
+++ b/solution.py
@@ -19,6 +19,7 @@
 PAIRS = 2
 FAR_PARTS = 2
 ENDS = 2 * SIDE * SIDE
+EARLY = 2
 TOP_CHUNK = 32
 AUX = 16
 
@@ -27,7 +28,7 @@
     per_group, tile,
     q_hbm, k_hbm, v_hbm, vert_hbm, slash_hbm, w_hbm, out_ref,
     q_ref, k_ref, v_ref, list_ref, vert_ref, slash_ref,
-    packs, slots, qg, qt, kg, vg, aux_k, places, w_ref, acc, top, far_top, total, o_buf, attn, give, take, out_buf,
+    packs, slots, qg, qt, kg, vg, aux_k, places, w_ref, acc, top, far_top, total, o_buf, attn, early, give, take, out_buf,
     in_sem, w_sem, pack_send, kv_send, kv_recv, q_send, q_recv, slot_recv, ring_send,
     o_send, o_recv, x_send, x_recv, out_sem,
 ):
@@ -411,10 +412,14 @@
 
     lax.fori_loop(0, SIDE, far_slab, 0)
     attn[c] = o_buf[c]
-    for d in range(1, SIDE):
+
+    def heads_in(d):
         for pair in range(PAIRS):
             there = attn.at[peer(d), :, pl.ds(pair * width // PAIRS, width // PAIRS)]
             remote(there, there, o_send.at[peer(d), pair], o_recv.at[peer(d), pair], next_plane).wait_recv()
+
+    for d in range(1, SIDE - 1):
+        heads_in(d)
 
     weight_copy.wait()
     tiles = give.shape[0]
@@ -432,12 +437,34 @@
         a = jnp.concatenate([attn[j, place, :] for j in range(SIDE)], axis=1)
         return jnp.dot(a, w_ref[:, columns], preferred_element_type=jnp.float32)
 
+    def from_peers(t, ds):
+        columns = pl.ds(pl.multiple_of(t * tile, tile), tile)
+        parts = [
+            jnp.dot(attn[peer(d), theirs, :], w_ref[lanes(peer(d), width), columns], preferred_element_type=jnp.float32)
+            for d in ds
+        ]
+        return functools.reduce(jnp.add, parts)
+
+    def early_share(t, _):
+        early[t] = from_peers(t, range(SIDE - 1))
+        return 0
+
+    lax.fori_loop(0, EARLY, early_share, 0)
+    heads_in(SIDE - 1)
+
+    def late_share(t, _):
+        give[t] = (early[t] + from_peers(t, (SIDE - 1,))).astype(jnp.bfloat16)
+        swap(t).start()
+        return 0
+
+    lax.fori_loop(0, EARLY, late_share, 0)
+
     def share(t, _):
         give[t] = project(t, theirs).astype(jnp.bfloat16)
         swap(t).start()
         return 0
 
-    lax.fori_loop(0, tiles, share, 0)
+    lax.fori_loop(EARLY, tiles, share, 0)
 
     def put(t):
         columns = pl.ds(pl.multiple_of(t * tile, tile), tile)
@@ -516,6 +543,7 @@
             pltpu.VMEM((SIDE, per_group, 1, rows), jnp.float32),
             pltpu.VMEM((SIDE, rows, width), jnp.bfloat16),
             pltpu.VMEM((SIDE, rows, width), jnp.bfloat16),
+            pltpu.VMEM((EARLY, rows // 2, tile), jnp.float32),
             pltpu.VMEM((tiles, rows // 2, tile), jnp.bfloat16),
             pltpu.VMEM((tiles, rows // 2, tile), jnp.bfloat16),
             pltpu.VMEM((rows // 2, model), jnp.bfloat16),

time: 68.8 us -> 68 us (0.988)
  no operation moved by 1% of the time
where the time goes in v6:
time: 68 us; the launch traced here: 67.8 us
  Pallas kernels  65.5 us (96%)
  local copies, waits for them, and re-layouts  2.29 us (3%)
    pallas_call x1, Pallas kernels, on_device(): pl.pallas_call(functools.partial(kernel, per_group, tile), out_shape=jax....  65.5 us
    unnamed x1, local copies, waits for them, and re-layouts  2.29 us

profile of v6, /device:TPU:7, one launch (start us, length us, event | category | flops | bytes accessed | tf_op | source)
XLA Modules:
  0.0 67.8 jit_solution(17801768049856242908)
XLA Ops:
  0.0 65.5 %shard_map.64 = bf16[128,4096]{1,0:T(8,128)(2,1)} custom-call(bf16[256,2048]{1,0:T(8,128)(2,1)} %q_hbm.1, bf16[256,512]{1,0:T(8,128)(2,1)} %k_hbm.1, bf16[256,512]{1,0:T(8,128)(2,1)} %v_hbm.1, s32[4,64]{1,0:T(4,128)} %vert_hbm.1, s32[2,4]{1,0:T(2,128)} %bitcast.1, bf16[2048,4096]{1,0:T(8,128)(2,1)} %w_hbm.1), custom_call_target="tpu_custom_call" | custom-call | tf_op jit(solution)/shard_map/pallas_call | solution.py:519
  65.5 2.3 %copy.8 = bf16[128,4096]{1,0:T(8,128)(2,1)} copy(bf16[128,4096]{1,0:T(8,128)(2,1)} %shard_map.64) | data formatting | bytes 2097152

commit v7 on v6

--- a/solution.py
+++ b/solution.py
@@ -345,8 +345,7 @@
             second(1, (2 + j) % SIDE)
             return 0
 
-        lax.fori_loop(jnp.where(step == 2, 1, jnp.where(step == 3, 0, SIDE)),
-                      jnp.where(step == 3, 1, SIDE), values_second, 0)
+        lax.fori_loop(jnp.where(step == 2, 0, SIDE), SIDE, values_second, 0)
         return 0
 
     lax.fori_loop(0, SIDE, first_pass, 0)

time: 68 us -> 67.9 us (level)
  the two profiles are of different devices: /device:TPU:7 before, /device:TPU:1 now
where the time goes in v7:
time: 67.9 us; the launch traced here: 67.7 us
  Pallas kernels  65.4 us (96%)
  local copies, waits for them, and re-layouts  2.29 us (3%)
    pallas_call x1, Pallas kernels, on_device(): pl.pallas_call(functools.partial(kernel, per_group, tile), out_shape=jax....  65.4 us
    unnamed x1, local copies, waits for them, and re-layouts  2.29 us

profile of v7, /device:TPU:1, one launch (start us, length us, event | category | flops | bytes accessed | tf_op | source)
XLA Modules:
  0.0 67.7 jit_solution(7270513820944733728)
XLA Ops:
  0.0 65.4 %shard_map.64 = bf16[128,4096]{1,0:T(8,128)(2,1)} custom-call(bf16[256,2048]{1,0:T(8,128)(2,1)} %q_hbm.1, bf16[256,512]{1,0:T(8,128)(2,1)} %k_hbm.1, bf16[256,512]{1,0:T(8,128)(2,1)} %v_hbm.1, s32[4,64]{1,0:T(4,128)} %vert_hbm.1, s32[2,4]{1,0:T(2,128)} %bitcast.1, bf16[2048,4096]{1,0:T(8,128)(2,1)} %w_hbm.1), custom_call_target="tpu_custom_call" | custom-call | tf_op jit(solution)/shard_map/pallas_call | solution.py:518
  65.4 2.3 %copy.8 = bf16[128,4096]{1,0:T(8,128)(2,1)} copy(bf16[128,4096]{1,0:T(8,128)(2,1)} %shard_map.64) | data formatting | bytes 2097152
